TPU v7x, 32 devices: a whole 2x2x4 slice. The times are simulated.
32 devices in a mesh: cfg: 2 (over x), ta: 16 (over z, y, core).
Axes of the slice: x: 2, y: 2, z: 4, core: 2. Of those that a mesh axis runs over, the one named last changes fastest.
Arguments:
- fine_source: bfloat16 [32, 128, 2, 2, 24, 128], P('cfg', 'ta'), parts along dimension 0, may hold values from -24 to 24
- projectors: bfloat16 [32, 128, 2304], P(('cfg', 'ta')), parts along dimension 0, may hold values from -0.21875 to 0.21875
- stencil_links: bfloat16 [32, 8, 48, 864], P(('cfg', 'ta')), parts along dimension 0, may hold values from -0.21875 to 0.21875
- quark_mass: float32 [2], P('cfg'), parts along dimension 0, may hold values from 1.5 to 3
Outputs:
- solution: float32 [32, 8, 96, 128], P(('cfg', 'ta')), parts along dimension 0
- residual: float32 [32, 8, 96, 128], P(('cfg', 'ta')), parts along dimension 0
There are 2 independent parts, one for each index of `cfg`. A program takes and returns all parts, laid end to end along the dimension named above; each array names one. Nothing has to cross between parts.
All inputs are finite; a program needn't handle non-finite values.
Results may differ from a plain program's by a relative error of at most 0.012.
The roundings to bfloat16 on the way count: a program that leaves them out, or rounds other values in their place, can miss the bound.
Values may be sent and summed in bfloat16 or wider, within the bound.
No kernel may reach another device: no remote copies, remote signals or barrier semaphores. Data moves between devices by JAX's collectives and lax.ppermute only.
A program may use at most 128 MiB of HBM per device.

v0:
```python
import math

import jax
import jax.numpy as jnp
from jax import lax
from jax.experimental import pallas as pl
from jax.experimental.pallas import tpu as pltpu
from jax.sharding import PartitionSpec as P


LX = 4
LZ = 8
ITERS = 3
LANES = 128
STEPS = (1, 3, 4, 7, 5, 6, 2)

VMEM = pl.BlockSpec(memory_space=pltpu.VMEM)
SMEM = pl.BlockSpec(memory_space=pltpu.SMEM)


def send(value, pairs):
    return lax.ppermute(value, "ta", pairs)


def whole_call(body, out_shape, operands, specs, scratch=()):
    return pl.pallas_call(
        body,
        out_shape=out_shape,
        in_specs=specs,
        out_specs=jax.tree.map(lambda _: VMEM, out_shape),
        scratch_shapes=list(scratch),
        compiler_params=pltpu.CompilerParams(vmem_limit_bytes=6 * 1024 * 1024),
    )(*operands)


def unpack_rows(values, rows_ref, pair_count, fine_count):
    column_count = values.shape[0]
    lane = lax.broadcasted_iota(jnp.int32, (column_count, LANES), 1)
    tiles = [values[:, t * LANES:(t + 1) * LANES] for t in range(values.shape[1] // LANES)]

    def window(start, target):
        tile, offset = divmod(start, LANES)
        shift = (target - offset) % LANES
        piece = pltpu.roll(tiles[tile], shift, 1) if shift else tiles[tile]
        if offset + fine_count > LANES:
            after = pltpu.roll(tiles[tile + 1], shift, 1) if shift else tiles[tile + 1]
            piece = jnp.where(lane < target + LANES - offset, piece, after)
        return piece

    for pair in range(pair_count):
        base = (pair * 2 // pair_count) * fine_count
        start = pair * 2 * fine_count
        first = window(start, base)
        second = window(start + fine_count, base + 2 * fine_count)
        row = jnp.where((lane >= base) & (lane < base + fine_count), first, 0.0)
        inside = (lane >= base + 2 * fine_count) & (lane < base + 3 * fine_count)
        row = jnp.where(inside, second, row)
        rows_ref[pl.ds(pair, column_count, stride=pair_count), :] = row


def step_order(chip_count):
    steps = list(range(1, chip_count))
    return list(STEPS) if sorted(STEPS) == steps else steps


def split_kernel(device_ref, proj_ref, *out_refs):
    chip = device_ref[0] // 2
    for step, out_ref in enumerate(out_refs):
        out_ref[...] = proj_ref[chip ^ step]


def restrict_kernel(step, device_ref, proj_ref, fine_ref, other_ref, source_ref, rows_ref):
    column_count = proj_ref.shape[0]
    local_count, comp_rows, rhs_count = fine_ref.shape[1:]
    half = comp_rows // 2
    fine_count = half // 2
    pair_count = proj_ref.shape[1] // (2 * fine_count)
    chip = (device_ref[0] // 2) ^ step
    parity = device_ref[0] % 2
    values = proj_ref[...].astype(jnp.float32)
    for core in range(column_count // local_count):
        unpack_rows(
            values[core * local_count:(core + 1) * local_count],
            rows_ref.at[core],
            pair_count,
            fine_count,
        )
    total = jnp.zeros((pair_count, 2 * rhs_count), jnp.float32)
    for core, ref, index in ((parity, fine_ref, 2 * chip + parity), (1 - parity, other_ref, chip)):
        for column in range(local_count):
            weights = rows_ref[core, pl.ds(column * pair_count, pair_count), :]
            weights = weights[:, :comp_rows].astype(jnp.bfloat16)
            block = ref[index, column]
            real, imag = block[:half], block[half:]
            right = jnp.concatenate(
                [
                    jnp.concatenate([real, imag], axis=1),
                    jnp.concatenate([imag, -real], axis=1),
                ],
                axis=0,
            )
            total = total + jnp.dot(weights, right, preferred_element_type=jnp.float32)
    source_ref[:pair_count] = total[:, :rhs_count]
    source_ref[pair_count:] = total[:, rhs_count:]


def join_kernel(steps, device_ref, *refs):
    parts, (source_ref, rounded_ref) = refs[:-2], refs[-2:]
    chip = device_ref[0] // 2
    for step, part in zip(steps, parts):
        source_ref[chip ^ step] = part[...]
        rounded_ref[chip ^ step] = part[...].astype(jnp.bfloat16)


def paired_restriction(fine_source, projectors, comp_count):
    plane_count, local_columns = fine_source.shape[:2]
    rhs_count = fine_source.shape[-1]
    width = projectors.shape[2]
    chip_count = plane_count // 2
    device = lax.axis_index("ta").astype(jnp.int32)
    place = device.reshape(1)
    low = jnp.bfloat16

    def swap(value, bits):
        return send(value, [(other, other ^ bits) for other in range(plane_count)])

    given = whole_call(
        split_kernel,
        [jax.ShapeDtypeStruct((2 * local_columns, width), low)] * chip_count,
        (place, projectors.reshape(chip_count, 2 * local_columns, width)),
        [SMEM, VMEM],
    )
    order = step_order(chip_count)
    moved = {0: given[0]}
    for step in order:
        moved[step] = swap(given[step], 2 * step)
    fine = fine_source.reshape(plane_count, local_columns, 2 * comp_count, rhs_count)
    halves = fine.reshape((chip_count, 2) + fine.shape[1:])
    other = swap(lax.dynamic_index_in_dim(halves, 1 - device % 2, axis=1, keepdims=False), 1)
    steps = order + [0]
    parts = {}
    for step in steps:
        part = whole_call(
            lambda *refs: restrict_kernel(step, *refs),
            jax.ShapeDtypeStruct((2 * comp_count, rhs_count), jnp.float32),
            (place, moved[step], fine, other),
            [SMEM, VMEM, VMEM, VMEM],
            [pltpu.VMEM((2, local_columns * comp_count, LANES), jnp.float32)],
        )
        parts[step] = swap(part, 2 * step) if step else part
    shape = (chip_count, 2 * comp_count, rhs_count)
    return whole_call(
        lambda *refs: join_kernel(steps, *refs),
        (jax.ShapeDtypeStruct(shape, jnp.float32), jax.ShapeDtypeStruct(shape, low)),
        (place, *(parts[step] for step in steps)),
        [SMEM] + [VMEM] * chip_count,
    )


def real_weights(proj_view):
    proj_re = proj_view[..., 0, :]
    proj_im = proj_view[..., 1, :]
    first_row = jnp.stack([proj_re, proj_im], axis=-4)
    second_row = jnp.stack([-proj_im, proj_re], axis=-4)
    return jnp.stack([first_row, second_row], axis=-5)


def general_restriction(fine_source, projectors, comp_count, site_count, block_count):
    null_count = comp_count // 2
    plane_count, local_columns = fine_source.shape[:2]
    fine_count, rhs_count = fine_source.shape[4:]
    moved_proj = lax.all_to_all(projectors, "ta", split_axis=1, concat_axis=0, tiled=True)
    group_size = math.gcd(block_count, local_columns)
    groups = local_columns // group_size
    weights = real_weights(
        moved_proj.reshape(plane_count, groups, group_size, 2, null_count, 2, fine_count)
    )
    fine_local = fine_source.reshape(plane_count, groups, group_size, 2, 2, fine_count, rhs_count)
    partial_sums = jnp.einsum(
        "pmgdchvk,pmgchkr->pmdhvr", weights, fine_local, preferred_element_type=jnp.float32
    )
    partial_sums = partial_sums.reshape(plane_count, groups, 2 * comp_count, rhs_count)
    collected = lax.all_to_all(partial_sums, "ta", split_axis=0, concat_axis=1, tiled=True)
    return jnp.sum(
        collected.reshape(site_count, block_count // group_size, 2 * comp_count, rhs_count), axis=1
    )


def fold(value):
    return jnp.sum(value.reshape(-1, 8, value.shape[-1]), axis=0)


def cross(left, right, half):
    left_re, left_im = left[:half], left[half:]
    right_re, right_im = right[:half], right[half:]
    return (
        fold(left_re * right_re + left_im * right_im),
        fold(left_re * right_im - left_im * right_re),
    )


def operator_kernel(count, mass_ref, links_ref, residual_ref, *refs):
    mapped_ref, sums_ref, packed_ref = refs[-3:]
    near = packed_ref.shape[0]
    nearby = refs[:near]
    basis = refs[near:near + count]
    site_count, comp_count, _ = links_ref.shape
    rhs_count = residual_ref.shape[2]
    line_count = site_count // LX
    mass = mass_ref[0]
    for number, vector in enumerate(nearby):
        for site in range(site_count):
            real = vector[site, :comp_count]
            imag = vector[site, comp_count:]
            packed_ref[number, site, :comp_count, :rhs_count] = real
            packed_ref[number, site, :comp_count, rhs_count:] = imag
            packed_ref[number, site, comp_count:, :rhs_count] = -imag
            packed_ref[number, site, comp_count:, rhs_count:] = real
    totals = [jnp.zeros((8, rhs_count), jnp.float32) for _ in range(3 + 2 * count)]
    for site in range(site_count):
        line, column = divmod(site, LX)
        places = [
            (0, line, column),
            (0, line, (column + 1) % LX),
            (0, line, (column - 1) % LX),
            (0, (line + 1) % line_count, column),
            (0, (line - 1) % line_count, column),
            (1, line, column),
            (2, line, column),
            (3, line, column),
            (near - 1, line, column),
        ]
        right = jnp.concatenate([packed_ref[n, y * LX + x] for n, y, x in places], axis=0)
        product = jnp.dot(links_ref[site], right, preferred_element_type=jnp.float32)
        own = nearby[0][site].astype(jnp.float32)
        mapped = (
            jnp.concatenate([product[:, :rhs_count], product[:, rhs_count:]], axis=0) + mass * own
        )
        mapped_ref[site] = mapped
        held = residual_ref[site]
        parts = [fold(mapped * mapped), *cross(mapped, held, comp_count)]
        for earlier in basis:
            parts += cross(earlier[site], mapped, comp_count)
        totals = [total + part for total, part in zip(totals, parts)]
    sums = jnp.concatenate(
        [jnp.sum(total, axis=0, keepdims=True) for total in totals]
        + [jnp.zeros((sums_ref.shape[-2] - len(totals), rhs_count), jnp.float32)],
        axis=0,
    )
    sums_ref[...] = sums


def scaled(vector, factor_re, factor_im, half):
    vector_re, vector_im = vector[:half], vector[half:]
    return jnp.concatenate(
        [
            factor_re * vector_re - factor_im * vector_im,
            factor_re * vector_im + factor_im * vector_re,
        ],
        axis=0,
    )


def times(left, right):
    return left[0] * right[0] - left[1] * right[1], left[0] * right[1] + left[1] * right[0]


def conj_times(left, right):
    return left[0] * right[0] + left[1] * right[1], left[0] * right[1] - left[1] * right[0]


def minus(left, right):
    return left[0] - right[0], left[1] - right[1]


def update_kernel(count, last, parts, *refs):
    refs = list(refs)
    part_refs = [refs.pop(0) for _ in range(parts)]
    mapped_ref, residual_ref = refs.pop(0), refs.pop(0)
    basis_q = [refs.pop(0) for _ in range(count)]
    basis_p = [refs.pop(0) for _ in range(count)]
    solution_ref, known_ref = (refs.pop(0), refs.pop(0)) if count else (None, None)
    if last:
        new_solution, new_residual = refs
    else:
        new_solution, new_residual, rounded_ref, unit_q_ref, unit_p_ref, new_known = refs
    site_count = mapped_ref.shape[0]
    half = mapped_ref.shape[1] // 2
    sums = add_pairs(part_refs)

    def row(ref, index):
        return ref[index:index + 1]

    squared = row(sums, 0)
    held_by_new = (row(sums, 1), row(sums, 2))
    coefs = [(row(sums, 3 + 2 * j), row(sums, 4 + 2 * j)) for j in range(count)]
    with_held = [(row(known_ref, 3 * j), row(known_ref, 3 * j + 1)) for j in range(count)]
    short = [row(known_ref, 3 * j + 2) for j in range(count)]
    pairs, place = {}, 3 * count
    for j in range(count):
        for i in range(j):
            pairs[i, j] = (row(known_ref, place), row(known_ref, place + 1))
            place += 2
    for j, coef in enumerate(coefs):
        size = coef[0] * coef[0] + coef[1] * coef[1]
        squared = squared - size * (1.0 + short[j])
        held_by_new = minus(held_by_new, conj_times(coef, with_held[j]))
        for i in range(j):
            squared = squared + 2.0 * conj_times(coefs[i], times(pairs[i, j], coef))[0]
    norm_square = squared + 1e-06
    factor = 1.0 / jnp.sqrt(norm_square)
    alpha = (held_by_new[0] * factor, held_by_new[1] * factor)
    if not last:
        with_new = []
        for j, coef in enumerate(coefs):
            left = (coef[0] * short[j], coef[1] * short[j])
            for i in range(count):
                if i != j:
                    pair = pairs[j, i] if j < i else (pairs[i, j][0], -pairs[i, j][1])
                    left = minus(left, times(pair, coefs[i]))
            with_new.append((left[0] * factor, left[1] * factor))
        new_short = 1e-06 / norm_square
        rows = []
        for j in range(count):
            rows += minus(with_held[j], times(with_new[j], alpha))
            rows.append(short[j])
        rows += [alpha[0] * new_short, alpha[1] * new_short, new_short]
        for j in range(count):
            for i in range(j):
                rows += pairs[i, j]
        for pair in with_new:
            rows += pair
        for index, value in enumerate(rows):
            new_known[index:index + 1] = value
    for site in range(site_count):
        mapped = mapped_ref[site]
        held = residual_ref[site]
        direction = held
        for number, (coef_re, coef_im) in enumerate(coefs):
            mapped = mapped - scaled(basis_q[number][site], coef_re, coef_im, half)
            direction = direction - scaled(basis_p[number][site], coef_re, coef_im, half)
        unit_q = mapped * factor
        unit_p = direction * factor
        change = scaled(unit_p, *alpha, half)
        new_solution[site] = change if solution_ref is None else solution_ref[site] + change
        held = held - scaled(unit_q, *alpha, half)
        new_residual[site] = held
        if not last:
            rounded_ref[site] = held.astype(jnp.bfloat16)
            unit_q_ref[site] = unit_q
            unit_p_ref[site] = unit_p


def add_pairs(refs):
    values = [ref[...] for ref in refs]
    while len(values) > 1:
        values = [values[i] + values[i + 1] for i in range(0, len(values), 2)]
    return values[0]


def add_kernel(*refs):
    refs[-1][...] = add_pairs(refs[:-1])


def gather_sums(sums, device_count):
    step = 1
    while step < device_count:
        step *= 4
    if step != device_count or device_count > 16:
        return [lax.psum(sums, "ta")]
    while step > 1:
        step //= 4
        parts = [sums]
        for turn in (1, 2, 3):
            pairs = [(device, device ^ (turn * step)) for device in range(device_count)]
            parts.append(send(sums, pairs))
        if step > 1:
            shape = jax.ShapeDtypeStruct(sums.shape, jnp.float32)
            sums = whole_call(add_kernel, shape, parts, [VMEM] * 4)
    return parts


def shards(fine_source, projectors, stencil_links, quark_mass):
    _, site_count, comp_count, _ = stencil_links.shape
    plane_count, local_columns = fine_source.shape[:2]
    rhs_count = fine_source.shape[5]
    block_count = projectors.shape[1] // site_count
    chip_count = plane_count // 2
    paired = local_columns * 2 == block_count and local_columns % 8 == 0
    if paired and chip_count & (chip_count - 1) == 0:
        source, rounded = paired_restriction(fine_source, projectors, comp_count)
    else:
        source = general_restriction(
            fine_source, projectors, comp_count, site_count, block_count
        )
        rounded = source.astype(jnp.bfloat16)
    links = stencil_links[0]
    ring = [
        (plane, plane // LZ * LZ + (plane + 1) % LZ) for plane in range(plane_count)
    ]
    back = [(target, origin) for origin, target in ring]
    later = [(plane, (plane + LZ) % plane_count) for plane in range(plane_count)]
    earlier = [(target, origin) for origin, target in later]

    def shape(*sizes, dtype=jnp.float32):
        return jax.ShapeDtypeStruct(sizes, dtype)

    width = 2 * comp_count
    full = shape(site_count, width, rhs_count)
    low = shape(site_count, width, rhs_count, dtype=jnp.bfloat16)
    residual = source
    total = None
    basis_q, basis_p = [], []
    for iteration in range(ITERS):
        last = iteration == ITERS - 1
        nearby = [rounded, send(rounded, back), send(rounded, ring)]
        nearby.append(send(rounded, earlier))
        if plane_count > 2 * LZ:
            nearby.append(send(rounded, later))
        operands = [quark_mass, links, residual, *nearby, *basis_q]
        mapped, sums = whole_call(
            lambda *refs: operator_kernel(iteration, *refs),
            (full, shape(-(-(3 + 2 * iteration) // 8) * 8, rhs_count)),
            operands,
            [SMEM] + [VMEM] * (len(operands) - 1),
            [pltpu.VMEM((len(nearby), site_count, width, 2 * rhs_count), jnp.bfloat16)],
        )
        parts = gather_sums(sums, plane_count)
        operands = [*parts, mapped, residual, *basis_q, *basis_p]
        if iteration:
            operands += [total, known]
        known_rows = -(-(3 * (iteration + 1) + iteration * (iteration + 1)) // 8) * 8
        results = (full, full)
        if not last:
            results += (low, full, full, shape(known_rows, rhs_count))
        outs = whole_call(
            lambda *refs: update_kernel(iteration, last, len(parts), *refs),
            results,
            operands,
            [VMEM] * len(operands),
        )
        total, residual = outs[:2]
        if not last:
            rounded, known = outs[2], outs[5]
            basis_q.append(outs[3])
            basis_p.append(outs[4])
    return total[None], residual[None]


def solution(mesh):
    return jax.shard_map(
        shards,
        mesh=mesh,
        in_specs=(
            P("cfg", "ta", None, None, None, None),
            P(("cfg", "ta"), None, None),
            P(("cfg", "ta"), None, None, None),
            P("cfg"),
        ),
        out_specs=(P(("cfg", "ta"), None, None, None), P(("cfg", "ta"), None, None, None)),
        check_vma=False,
    )
```

profile of v0, /device:TPU:0, one launch (start us, length us, event | category | flops | bytes accessed | tf_op | source)
XLA Modules:
  0.0 103.5 jit_solution(13708013405049333097)
XLA Ops:
  0.7 1.7 %dynamic-slice_bitcast_fusion = bf16[8,8,96,128]{3,2,1,0:T(8,128)(2,1)S(1)} fusion(bf16[8,2,8,96,128]{4,3,2,1,0:T(8,128)(2,1)} %bitcast.11, s32[]{:T(128)S(6)} %select_n.12), kind=kLoop, calls=%fused_computation | loop fusion | bytes 3145732 | tf_op jit(solution)/shard_map/jit(dynamic_index_in_dim)/squeeze | solution.py:139
  3.0 2.6 %collective-permute-start = (bf16[16,2304]{1,0:T(8,128)(2,1)S(1)}, bf16[16,2304]{1,0:T(8,128)(2,1)S(1)}, u32[]{:S(2)}, u32[]{:S(2)}) collective-permute-start(bf16[16,2304]{1,0:T(8,128)(2,1)S(1)} %get-tuple-element.32), channel_id=1, source_target_pairs={{0,2},{1,3},{2,0},{3,1},{4,6},{5,7},{6,4},{7,5},{8,10},{9,11},{10,... | collective-permute-start | bytes 221192 | tf_op jit(solution)/shard_map/ppermute | solution.py:22
  7.1 2.6 %collective-permute-start.5 = (bf16[16,2304]{1,0:T(8,128)(2,1)S(1)}, bf16[16,2304]{1,0:T(8,128)(2,1)S(1)}, u32[]{:S(2)}, u32[]{:S(2)}) collective-permute-start(bf16[16,2304]{1,0:T(8,128)(2,1)S(1)} %get-tuple-element.34), channel_id=1, source_target_pairs={{0,8},{1,9},{2,10},{3,11},{4,12},{5,13},{6,14},{7,15},{8,0},{9,1},... | collective-permute-start | bytes 221192 | tf_op jit(solution)/shard_map/ppermute | solution.py:22
  10.1 4.1 %collective-permute-start.7 = (bf16[16,2304]{1,0:T(8,128)(2,1)S(1)}, bf16[16,2304]{1,0:T(8,128)(2,1)S(1)}, u32[]{:S(2)}, u32[]{:S(2)}) collective-permute-start(bf16[16,2304]{1,0:T(8,128)(2,1)S(1)} %get-tuple-element.35), channel_id=1, source_target_pairs={{0,14},{1,15},{2,12},{3,13},{4,10},{5,11},{6,8},{7,9},{8,6},{9,7},... | collective-permute-start | bytes 221192 | tf_op jit(solution)/shard_map/ppermute | solution.py:22
  14.2 1.9 %collective-permute-start.11 = (bf16[16,2304]{1,0:T(8,128)(2,1)S(1)}, bf16[16,2304]{1,0:T(8,128)(2,1)S(1)}, u32[]{:S(2)}, u32[]{:S(2)}) collective-permute-start(bf16[16,2304]{1,0:T(8,128)(2,1)S(1)} %get-tuple-element.37), channel_id=1, source_target_pairs={{0,12},{1,13},{2,14},{3,15},{4,8},{5,9},{6,10},{7,11},{8,4},{9,5},... | collective-permute-start | bytes 221192 | tf_op jit(solution)/shard_map/ppermute | solution.py:22
  17.1 1.8 %collective-permute-start.2 = (f32[96,128]{1,0:T(8,128)S(1)}, f32[96,128]{1,0:T(8,128)S(1)}, u32[]{:S(2)}, u32[]{:S(2)}) collective-permute-start(f32[96,128]{1,0:T(8,128)S(1)} %shard_map.60), channel_id=1, source_target_pairs={{0,2},{1,3},{2,0},{3,1},{4,6},{5,7},{6,4},{7,5},{8,10},{9,11},{10,... | collective-permute-start | bytes 147464 | tf_op jit(solution)/shard_map/ppermute | solution.py:22
  20.7 2.8 %collective-permute-start.6 = (f32[96,128]{1,0:T(8,128)S(1)}, f32[96,128]{1,0:T(8,128)S(1)}, u32[]{:S(2)}, u32[]{:S(2)}) collective-permute-start(f32[96,128]{1,0:T(8,128)S(1)} %shard_map.62), channel_id=1, source_target_pairs={{0,8},{1,9},{2,10},{3,11},{4,12},{5,13},{6,14},{7,15},{8,0},{9,1},... | collective-permute-start | bytes 147464 | tf_op jit(solution)/shard_map/ppermute | solution.py:22
  24.0 2.1 %collective-permute-start.8 = (f32[96,128]{1,0:T(8,128)S(1)}, f32[96,128]{1,0:T(8,128)S(1)}, u32[]{:S(2)}, u32[]{:S(2)}) collective-permute-start(f32[96,128]{1,0:T(8,128)S(1)} %shard_map.63), channel_id=1, source_target_pairs={{0,14},{1,15},{2,12},{3,13},{4,10},{5,11},{6,8},{7,9},{8,6},{9,7},... | collective-permute-start | bytes 147464 | tf_op jit(solution)/shard_map/ppermute | solution.py:22
  29.3 2.7 %collective-permute-start.14 = (f32[96,128]{1,0:T(8,128)S(1)}, f32[96,128]{1,0:T(8,128)S(1)}, u32[]{:S(2)}, u32[]{:S(2)}) collective-permute-start(f32[96,128]{1,0:T(8,128)S(1)} %shard_map.66), channel_id=1, source_target_pairs={{0,4},{1,5},{2,6},{3,7},{4,0},{5,1},{6,2},{7,3},{8,12},{9,13},{10,... | collective-permute-start | bytes 147464 | tf_op jit(solution)/shard_map/ppermute | solution.py:22
  34.4 1.7 %collective-permute-start.17 = (bf16[8,96,128]{2,1,0:T(8,128)(2,1)S(1)}, bf16[8,96,128]{2,1,0:T(8,128)(2,1)S(1)}, u32[]{:S(2)}, u32[]{:S(2)}) collective-permute-start(bf16[8,96,128]{2,1,0:T(8,128)(2,1)S(1)} %get-tuple-element.41.refs_3_), channel_id=1, source_target_pairs={{8,0},{9,1},{10,2},{11,3},{12,4},{13,5},{14,6},{15,7},{0,8},{1,9},... | collective-permute-start | bytes 589832 | tf_op jit(solution)/shard_map/ppermute | solution.py:22
  36.1 2.6 %collective-permute-start.15 = (bf16[8,96,128]{2,1,0:T(8,128)(2,1)S(1)}, bf16[8,96,128]{2,1,0:T(8,128)(2,1)S(1)}, u32[]{:S(2)}, u32[]{:S(2)}) collective-permute-start(bf16[8,96,128]{2,1,0:T(8,128)(2,1)S(1)} %get-tuple-element.41.refs_3_), channel_id=1, source_target_pairs={{1,0},{2,1},{3,2},{4,3},{5,4},{6,5},{7,6},{0,7},{9,8},{10,9},{11,1... | collective-permute-start | bytes 589832 | tf_op jit(solution)/shard_map/ppermute | solution.py:22
  39.4 4.0 %collective-permute-done.17.refs_6_ = bf16[8,96,128]{2,1,0:T(8,128)(2,1)S(1)} collective-permute-done((bf16[8,96,128]{2,1,0:T(8,128)(2,1)S(1)}, bf16[8,96,128]{2,1,0:T(8,128)(2,1)S(1)}, u32[]{:S(2)}, u32[]{:S(2)}) %collective-permute-start.17) | collective-permute-done | bytes 196640 | tf_op jit(solution)/shard_map/ppermute | solution.py:22
  45.0 2.5 %collective-permute-start.20 = (f32[8,128]{1,0:T(8,128)S(1)}, f32[8,128]{1,0:T(8,128)S(1)}, u32[]{:S(2)}, u32[]{:S(2)}) collective-permute-start(f32[8,128]{1,0:T(8,128)S(1)} %get-tuple-element.42.refs_0_), channel_id=1, source_target_pairs={{0,12},{1,13},{2,14},{3,15},{4,8},{5,9},{6,10},{7,11},{8,4},{9,5},... | collective-permute-start | bytes 12296 | tf_op jit(solution)/shard_map/ppermute | solution.py:22
  47.5 2.0 %collective-permute-start.18 = (f32[8,128]{1,0:T(8,128)S(1)}, f32[8,128]{1,0:T(8,128)S(1)}, u32[]{:S(2)}, u32[]{:S(2)}) collective-permute-start(f32[8,128]{1,0:T(8,128)S(1)} %get-tuple-element.42.refs_0_), channel_id=1, source_target_pairs={{0,4},{1,5},{2,6},{3,7},{4,0},{5,1},{6,2},{7,3},{8,12},{9,13},{10,... | collective-permute-start | bytes 12296 | tf_op jit(solution)/shard_map/ppermute | solution.py:22
  52.2 1.8 %collective-permute-start.21 = (f32[8,128]{1,0:T(8,128)S(1)}, f32[8,128]{1,0:T(8,128)S(1)}, u32[]{:S(2)}, u32[]{:S(2)}) collective-permute-start(f32[8,128]{1,0:T(8,128)S(1)} %shard_map.70.refs_0_), channel_id=1, source_target_pairs={{0,1},{1,0},{2,3},{3,2},{4,5},{5,4},{6,7},{7,6},{8,9},{9,8},{10,11... | collective-permute-start | bytes 12296 | tf_op jit(solution)/shard_map/ppermute | solution.py:22
  56.0 2.0 %collective-permute-start.26 = (bf16[8,96,128]{2,1,0:T(8,128)(2,1)S(1)}, bf16[8,96,128]{2,1,0:T(8,128)(2,1)S(1)}, u32[]{:S(2)}, u32[]{:S(2)}) collective-permute-start(bf16[8,96,128]{2,1,0:T(8,128)(2,1)S(1)} %get-tuple-element.45.refs_3_), channel_id=1, source_target_pairs={{8,0},{9,1},{10,2},{11,3},{12,4},{13,5},{14,6},{15,7},{0,8},{1,9},... | collective-permute-start | bytes 589832 | tf_op jit(solution)/shard_map/ppermute | solution.py:22
  58.0 2.6 %collective-permute-start.24 = (bf16[8,96,128]{2,1,0:T(8,128)(2,1)S(1)}, bf16[8,96,128]{2,1,0:T(8,128)(2,1)S(1)}, u32[]{:S(2)}, u32[]{:S(2)}) collective-permute-start(bf16[8,96,128]{2,1,0:T(8,128)(2,1)S(1)} %get-tuple-element.45.refs_3_), channel_id=1, source_target_pairs={{1,0},{2,1},{3,2},{4,3},{5,4},{6,5},{7,6},{0,7},{9,8},{10,9},{11,1... | collective-permute-start | bytes 589832 | tf_op jit(solution)/shard_map/ppermute | solution.py:22
  60.6 6.9 %collective-permute-done.26.refs_6_ = bf16[8,96,128]{2,1,0:T(8,128)(2,1)S(1)} collective-permute-done((bf16[8,96,128]{2,1,0:T(8,128)(2,1)S(1)}, bf16[8,96,128]{2,1,0:T(8,128)(2,1)S(1)}, u32[]{:S(2)}, u32[]{:S(2)}) %collective-permute-start.26) | collective-permute-done | bytes 196640 | tf_op jit(solution)/shard_map/ppermute | solution.py:22
  69.9 2.9 %collective-permute-start.27 = (f32[8,128]{1,0:T(8,128)S(1)}, f32[8,128]{1,0:T(8,128)S(1)}, u32[]{:S(2)}, u32[]{:S(2)}) collective-permute-start(f32[8,128]{1,0:T(8,128)S(1)} %get-tuple-element.47.refs_0_), channel_id=1, source_target_pairs={{0,4},{1,5},{2,6},{3,7},{4,0},{5,1},{6,2},{7,3},{8,12},{9,13},{10,... | collective-permute-start | bytes 12296 | tf_op jit(solution)/shard_map/ppermute | solution.py:22
  78.6 1.9 %collective-permute-start.35 = (bf16[8,96,128]{2,1,0:T(8,128)(2,1)S(1)}, bf16[8,96,128]{2,1,0:T(8,128)(2,1)S(1)}, u32[]{:S(2)}, u32[]{:S(2)}) collective-permute-start(bf16[8,96,128]{2,1,0:T(8,128)(2,1)S(1)} %get-tuple-element.53.refs_3_), channel_id=1, source_target_pairs={{8,0},{9,1},{10,2},{11,3},{12,4},{13,5},{14,6},{15,7},{0,8},{1,9},... | collective-permute-start | bytes 589832 | tf_op jit(solution)/shard_map/ppermute | solution.py:22
  80.4 2.6 %collective-permute-start.33 = (bf16[8,96,128]{2,1,0:T(8,128)(2,1)S(1)}, bf16[8,96,128]{2,1,0:T(8,128)(2,1)S(1)}, u32[]{:S(2)}, u32[]{:S(2)}) collective-permute-start(bf16[8,96,128]{2,1,0:T(8,128)(2,1)S(1)} %get-tuple-element.53.refs_3_), channel_id=1, source_target_pairs={{1,0},{2,1},{3,2},{4,3},{5,4},{6,5},{7,6},{0,7},{9,8},{10,9},{11,1... | collective-permute-start | bytes 589832 | tf_op jit(solution)/shard_map/ppermute | solution.py:22
  83.1 7.6 %collective-permute-done.35.refs_6_ = bf16[8,96,128]{2,1,0:T(8,128)(2,1)S(1)} collective-permute-done((bf16[8,96,128]{2,1,0:T(8,128)(2,1)S(1)}, bf16[8,96,128]{2,1,0:T(8,128)(2,1)S(1)}, u32[]{:S(2)}, u32[]{:S(2)}) %collective-permute-start.35) | collective-permute-done | bytes 196640 | tf_op jit(solution)/shard_map/ppermute | solution.py:22
  91.6 2.5 %collective-permute-start.38 = (f32[8,128]{1,0:T(8,128)S(1)}, f32[8,128]{1,0:T(8,128)S(1)}, u32[]{:S(2)}, u32[]{:S(2)}) collective-permute-start(f32[8,128]{1,0:T(8,128)S(1)} %get-tuple-element.55.refs_0_), channel_id=1, source_target_pairs={{0,12},{1,13},{2,14},{3,15},{4,8},{5,9},{6,10},{7,11},{8,4},{9,5},... | collective-permute-start | bytes 12296 | tf_op jit(solution)/shard_map/ppermute | solution.py:22
  94.0 2.0 %collective-permute-start.36 = (f32[8,128]{1,0:T(8,128)S(1)}, f32[8,128]{1,0:T(8,128)S(1)}, u32[]{:S(2)}, u32[]{:S(2)}) collective-permute-start(f32[8,128]{1,0:T(8,128)S(1)} %get-tuple-element.55.refs_0_), channel_id=1, source_target_pairs={{0,4},{1,5},{2,6},{3,7},{4,0},{5,1},{6,2},{7,3},{8,12},{9,13},{10,... | collective-permute-start | bytes 12296 | tf_op jit(solution)/shard_map/ppermute | solution.py:22
  (86 shorter events, 34.2 us)
Async XLA Ops:
  2.3 11.9 %collective-permute-start.1 = (bf16[8,8,96,128]{3,2,1,0:T(8,128)(2,1)S(1)}, bf16[8,8,96,128]{3,2,1,0:T(8,128)(2,1)S(1)}, u32[]{:S(2)}, u32[]{:S(2)}) collective-permute-start(bf16[8,8,96,128]{3,2,1,0:T(8,128)(2,1)S(1)} %dynamic-slice_bitcast_fusion), channel_id=1, source_target_pairs={{0,1},{1,0},{2,3},{3,2},{4,5},{5,4},{6,7},{7,6},{8,9},{9,8},{10,11... | collective-permute-start | bytes 4718600 | tf_op jit(solution)/shard_map/ppermute | solution.py:22
  3.0 7.2 %collective-permute-start = (bf16[16,2304]{1,0:T(8,128)(2,1)S(1)}, bf16[16,2304]{1,0:T(8,128)(2,1)S(1)}, u32[]{:S(2)}, u32[]{:S(2)}) collective-permute-start(bf16[16,2304]{1,0:T(8,128)(2,1)S(1)} %get-tuple-element.32), channel_id=1, source_target_pairs={{0,2},{1,3},{2,0},{3,1},{4,6},{5,7},{6,4},{7,5},{8,10},{9,11},{10,... | collective-permute-start | bytes 221192 | tf_op jit(solution)/shard_map/ppermute | solution.py:22
  5.6 8.7 %collective-permute-start.3 = (bf16[16,2304]{1,0:T(8,128)(2,1)S(1)}, bf16[16,2304]{1,0:T(8,128)(2,1)S(1)}, u32[]{:S(2)}, u32[]{:S(2)}) collective-permute-start(bf16[16,2304]{1,0:T(8,128)(2,1)S(1)} %get-tuple-element.33), channel_id=1, source_target_pairs={{0,6},{1,7},{2,4},{3,5},{4,2},{5,3},{6,0},{7,1},{8,14},{9,15},{10,... | collective-permute-start | bytes 221192 | tf_op jit(solution)/shard_map/ppermute | solution.py:22
  7.1 10.1 %collective-permute-start.5 = (bf16[16,2304]{1,0:T(8,128)(2,1)S(1)}, bf16[16,2304]{1,0:T(8,128)(2,1)S(1)}, u32[]{:S(2)}, u32[]{:S(2)}) collective-permute-start(bf16[16,2304]{1,0:T(8,128)(2,1)S(1)} %get-tuple-element.34), channel_id=1, source_target_pairs={{0,8},{1,9},{2,10},{3,11},{4,12},{5,13},{6,14},{7,15},{8,0},{9,1},... | collective-permute-start | bytes 221192 | tf_op jit(solution)/shard_map/ppermute | solution.py:22
  9.7 9.2 %collective-permute-start.13 = (bf16[16,2304]{1,0:T(8,128)(2,1)S(1)}, bf16[16,2304]{1,0:T(8,128)(2,1)S(1)}, u32[]{:S(2)}, u32[]{:S(2)}) collective-permute-start(bf16[16,2304]{1,0:T(8,128)(2,1)S(1)} %get-tuple-element.38), channel_id=1, source_target_pairs={{0,4},{1,5},{2,6},{3,7},{4,0},{5,1},{6,2},{7,3},{8,12},{9,13},{10,... | collective-permute-start | bytes 221192 | tf_op jit(solution)/shard_map/ppermute | solution.py:22
  10.1 10.5 %collective-permute-start.7 = (bf16[16,2304]{1,0:T(8,128)(2,1)S(1)}, bf16[16,2304]{1,0:T(8,128)(2,1)S(1)}, u32[]{:S(2)}, u32[]{:S(2)}) collective-permute-start(bf16[16,2304]{1,0:T(8,128)(2,1)S(1)} %get-tuple-element.35), channel_id=1, source_target_pairs={{0,14},{1,15},{2,12},{3,13},{4,10},{5,11},{6,8},{7,9},{8,6},{9,7},... | collective-permute-start | bytes 221192 | tf_op jit(solution)/shard_map/ppermute | solution.py:22
  14.2 9.7 %collective-permute-start.9 = (bf16[16,2304]{1,0:T(8,128)(2,1)S(1)}, bf16[16,2304]{1,0:T(8,128)(2,1)S(1)}, u32[]{:S(2)}, u32[]{:S(2)}) collective-permute-start(bf16[16,2304]{1,0:T(8,128)(2,1)S(1)} %get-tuple-element.36), channel_id=1, source_target_pairs={{0,10},{1,11},{2,8},{3,9},{4,14},{5,15},{6,12},{7,13},{8,2},{9,3},... | collective-permute-start | bytes 221192 | tf_op jit(solution)/shard_map/ppermute | solution.py:22
  14.2 12.3 %collective-permute-start.11 = (bf16[16,2304]{1,0:T(8,128)(2,1)S(1)}, bf16[16,2304]{1,0:T(8,128)(2,1)S(1)}, u32[]{:S(2)}, u32[]{:S(2)}) collective-permute-start(bf16[16,2304]{1,0:T(8,128)(2,1)S(1)} %get-tuple-element.37), channel_id=1, source_target_pairs={{0,12},{1,13},{2,14},{3,15},{4,8},{5,9},{6,10},{7,11},{8,4},{9,5},... | collective-permute-start | bytes 221192 | tf_op jit(solution)/shard_map/ppermute | solution.py:22
  17.1 10.7 %collective-permute-start.2 = (f32[96,128]{1,0:T(8,128)S(1)}, f32[96,128]{1,0:T(8,128)S(1)}, u32[]{:S(2)}, u32[]{:S(2)}) collective-permute-start(f32[96,128]{1,0:T(8,128)S(1)} %shard_map.60), channel_id=1, source_target_pairs={{0,2},{1,3},{2,0},{3,1},{4,6},{5,7},{6,4},{7,5},{8,10},{9,11},{10,... | collective-permute-start | bytes 147464 | tf_op jit(solution)/shard_map/ppermute | solution.py:22
  18.9 10.4 %collective-permute-start.4 = (f32[96,128]{1,0:T(8,128)S(1)}, f32[96,128]{1,0:T(8,128)S(1)}, u32[]{:S(2)}, u32[]{:S(2)}) collective-permute-start(f32[96,128]{1,0:T(8,128)S(1)} %shard_map.61), channel_id=1, source_target_pairs={{0,6},{1,7},{2,4},{3,5},{4,2},{5,3},{6,0},{7,1},{8,14},{9,15},{10,... | collective-permute-start | bytes 147464 | tf_op jit(solution)/shard_map/ppermute | solution.py:22
  20.7 11.8 %collective-permute-start.6 = (f32[96,128]{1,0:T(8,128)S(1)}, f32[96,128]{1,0:T(8,128)S(1)}, u32[]{:S(2)}, u32[]{:S(2)}) collective-permute-start(f32[96,128]{1,0:T(8,128)S(1)} %shard_map.62), channel_id=1, source_target_pairs={{0,8},{1,9},{2,10},{3,11},{4,12},{5,13},{6,14},{7,15},{8,0},{9,1},... | collective-permute-start | bytes 147464 | tf_op jit(solution)/shard_map/ppermute | solution.py:22
  24.0 8.5 %collective-permute-start.8 = (f32[96,128]{1,0:T(8,128)S(1)}, f32[96,128]{1,0:T(8,128)S(1)}, u32[]{:S(2)}, u32[]{:S(2)}) collective-permute-start(f32[96,128]{1,0:T(8,128)S(1)} %shard_map.63), channel_id=1, source_target_pairs={{0,14},{1,15},{2,12},{3,13},{4,10},{5,11},{6,8},{7,9},{8,6},{9,7},... | collective-permute-start | bytes 147464 | tf_op jit(solution)/shard_map/ppermute | solution.py:22
  26.6 6.3 %collective-permute-start.10 = (f32[96,128]{1,0:T(8,128)S(1)}, f32[96,128]{1,0:T(8,128)S(1)}, u32[]{:S(2)}, u32[]{:S(2)}) collective-permute-start(f32[96,128]{1,0:T(8,128)S(1)} %shard_map.64), channel_id=1, source_target_pairs={{0,10},{1,11},{2,8},{3,9},{4,14},{5,15},{6,12},{7,13},{8,2},{9,3},... | collective-permute-start | bytes 147464 | tf_op jit(solution)/shard_map/ppermute | solution.py:22
  27.9 6.1 %collective-permute-start.12 = (f32[96,128]{1,0:T(8,128)S(1)}, f32[96,128]{1,0:T(8,128)S(1)}, u32[]{:S(2)}, u32[]{:S(2)}) collective-permute-start(f32[96,128]{1,0:T(8,128)S(1)} %shard_map.65), channel_id=1, source_target_pairs={{0,12},{1,13},{2,14},{3,15},{4,8},{5,9},{6,10},{7,11},{8,4},{9,5},... | collective-permute-start | bytes 147464 | tf_op jit(solution)/shard_map/ppermute | solution.py:22
  34.4 9.0 %collective-permute-start.17 = (bf16[8,96,128]{2,1,0:T(8,128)(2,1)S(1)}, bf16[8,96,128]{2,1,0:T(8,128)(2,1)S(1)}, u32[]{:S(2)}, u32[]{:S(2)}) collective-permute-start(bf16[8,96,128]{2,1,0:T(8,128)(2,1)S(1)} %get-tuple-element.41.refs_3_), channel_id=1, source_target_pairs={{8,0},{9,1},{10,2},{11,3},{12,4},{13,5},{14,6},{15,7},{0,8},{1,9},... | collective-permute-start | bytes 589832 | tf_op jit(solution)/shard_map/ppermute | solution.py:22
  36.1 8.1 %collective-permute-start.16 = (bf16[8,96,128]{2,1,0:T(8,128)(2,1)S(1)}, bf16[8,96,128]{2,1,0:T(8,128)(2,1)S(1)}, u32[]{:S(2)}, u32[]{:S(2)}) collective-permute-start(bf16[8,96,128]{2,1,0:T(8,128)(2,1)S(1)} %get-tuple-element.41.refs_3_), channel_id=1, source_target_pairs={{0,1},{1,2},{2,3},{3,4},{4,5},{5,6},{6,7},{7,0},{8,9},{9,10},{10,1... | collective-permute-start | bytes 589832 | tf_op jit(solution)/shard_map/ppermute | solution.py:22
  36.1 8.1 %collective-permute-start.15 = (bf16[8,96,128]{2,1,0:T(8,128)(2,1)S(1)}, bf16[8,96,128]{2,1,0:T(8,128)(2,1)S(1)}, u32[]{:S(2)}, u32[]{:S(2)}) collective-permute-start(bf16[8,96,128]{2,1,0:T(8,128)(2,1)S(1)} %get-tuple-element.41.refs_3_), channel_id=1, source_target_pairs={{1,0},{2,1},{3,2},{4,3},{5,4},{6,5},{7,6},{0,7},{9,8},{10,9},{11,1... | collective-permute-start | bytes 589832 | tf_op jit(solution)/shard_map/ppermute | solution.py:22
  45.0 5.5 %collective-permute-start.20 = (f32[8,128]{1,0:T(8,128)S(1)}, f32[8,128]{1,0:T(8,128)S(1)}, u32[]{:S(2)}, u32[]{:S(2)}) collective-permute-start(f32[8,128]{1,0:T(8,128)S(1)} %get-tuple-element.42.refs_0_), channel_id=1, source_target_pairs={{0,12},{1,13},{2,14},{3,15},{4,8},{5,9},{6,10},{7,11},{8,4},{9,5},... | collective-permute-start | bytes 12296 | tf_op jit(solution)/shard_map/ppermute | solution.py:22
  56.0 11.5 %collective-permute-start.26 = (bf16[8,96,128]{2,1,0:T(8,128)(2,1)S(1)}, bf16[8,96,128]{2,1,0:T(8,128)(2,1)S(1)}, u32[]{:S(2)}, u32[]{:S(2)}) collective-permute-start(bf16[8,96,128]{2,1,0:T(8,128)(2,1)S(1)} %get-tuple-element.45.refs_3_), channel_id=1, source_target_pairs={{8,0},{9,1},{10,2},{11,3},{12,4},{13,5},{14,6},{15,7},{0,8},{1,9},... | collective-permute-start | bytes 589832 | tf_op jit(solution)/shard_map/ppermute | solution.py:22
  58.0 9.5 %collective-permute-start.25 = (bf16[8,96,128]{2,1,0:T(8,128)(2,1)S(1)}, bf16[8,96,128]{2,1,0:T(8,128)(2,1)S(1)}, u32[]{:S(2)}, u32[]{:S(2)}) collective-permute-start(bf16[8,96,128]{2,1,0:T(8,128)(2,1)S(1)} %get-tuple-element.45.refs_3_), channel_id=1, source_target_pairs={{0,1},{1,2},{2,3},{3,4},{4,5},{5,6},{6,7},{7,0},{8,9},{9,10},{10,1... | collective-permute-start | bytes 589832 | tf_op jit(solution)/shard_map/ppermute | solution.py:22
  58.0 9.5 %collective-permute-start.24 = (bf16[8,96,128]{2,1,0:T(8,128)(2,1)S(1)}, bf16[8,96,128]{2,1,0:T(8,128)(2,1)S(1)}, u32[]{:S(2)}, u32[]{:S(2)}) collective-permute-start(bf16[8,96,128]{2,1,0:T(8,128)(2,1)S(1)} %get-tuple-element.45.refs_3_), channel_id=1, source_target_pairs={{1,0},{2,1},{3,2},{4,3},{5,4},{6,5},{7,6},{0,7},{9,8},{10,9},{11,1... | collective-permute-start | bytes 589832 | tf_op jit(solution)/shard_map/ppermute | solution.py:22
  78.6 12.1 %collective-permute-start.35 = (bf16[8,96,128]{2,1,0:T(8,128)(2,1)S(1)}, bf16[8,96,128]{2,1,0:T(8,128)(2,1)S(1)}, u32[]{:S(2)}, u32[]{:S(2)}) collective-permute-start(bf16[8,96,128]{2,1,0:T(8,128)(2,1)S(1)} %get-tuple-element.53.refs_3_), channel_id=1, source_target_pairs={{8,0},{9,1},{10,2},{11,3},{12,4},{13,5},{14,6},{15,7},{0,8},{1,9},... | collective-permute-start | bytes 589832 | tf_op jit(solution)/shard_map/ppermute | solution.py:22
  80.4 10.2 %collective-permute-start.34 = (bf16[8,96,128]{2,1,0:T(8,128)(2,1)S(1)}, bf16[8,96,128]{2,1,0:T(8,128)(2,1)S(1)}, u32[]{:S(2)}, u32[]{:S(2)}) collective-permute-start(bf16[8,96,128]{2,1,0:T(8,128)(2,1)S(1)} %get-tuple-element.53.refs_3_), channel_id=1, source_target_pairs={{0,1},{1,2},{2,3},{3,4},{4,5},{5,6},{6,7},{7,0},{8,9},{9,10},{10,1... | collective-permute-start | bytes 589832 | tf_op jit(solution)/shard_map/ppermute | solution.py:22
  80.4 10.2 %collective-permute-start.33 = (bf16[8,96,128]{2,1,0:T(8,128)(2,1)S(1)}, bf16[8,96,128]{2,1,0:T(8,128)(2,1)S(1)}, u32[]{:S(2)}, u32[]{:S(2)}) collective-permute-start(bf16[8,96,128]{2,1,0:T(8,128)(2,1)S(1)} %get-tuple-element.53.refs_3_), channel_id=1, source_target_pairs={{1,0},{2,1},{3,2},{4,3},{5,4},{6,5},{7,6},{0,7},{9,8},{10,9},{11,1... | collective-permute-start | bytes 589832 | tf_op jit(solution)/shard_map/ppermute | solution.py:22
  (21 other events, 102.2 us)
where the time goes:
time: 104 us
  starting transfers between devices  58.8 us (57%)
  waiting for transfers between devices  33.5 us (32%)
  Pallas kernels  8.04 us (8%)
  local copies, waits for them, and re-layouts  1.69 us (2%)
  between operations  1.55 us (1%)
    ppermute x42, starting transfers between devices, send(): return lax.ppermute(value, 'ta', pairs)  58.8 us
    ppermute x42, waiting for transfers between devices, send(): return lax.ppermute(value, 'ta', pairs)  33.5 us
    pallas_call x19, Pallas kernels, whole_call(): pl.pallas_call(body, out_shape=out_shape, in_specs=specs, out_specs=jax.t...  8.04 us
  transfers between devices with their start and end apart: 42, of which 20 were waited for; matrix products, arithmetic and copies ran while one was open for 0% of the time, Pallas kernels for 4%

commit v1 on v0

--- a/solution.py
+++ b/solution.py
@@ -12,7 +12,8 @@
 LZ = 8
 ITERS = 3
 LANES = 128
-STEPS = (1, 3, 4, 7, 5, 6, 2)
+PROJ_STEPS = (6, 3, 7, 1, 5, 2, 4)
+SOURCE_STEPS = (6, 3, 7, 5, 4, 1, 2)
 
 VMEM = pl.BlockSpec(memory_space=pltpu.VMEM)
 SMEM = pl.BlockSpec(memory_space=pltpu.SMEM)
@@ -58,9 +59,9 @@
         rows_ref[pl.ds(pair, column_count, stride=pair_count), :] = row
 
 
-def step_order(chip_count):
+def step_order(chip_count, wanted):
     steps = list(range(1, chip_count))
-    return list(STEPS) if sorted(STEPS) == steps else steps
+    return list(wanted) if sorted(wanted) == steps else steps
 
 
 def split_kernel(device_ref, proj_ref, *out_refs):
@@ -130,14 +131,14 @@
         (place, projectors.reshape(chip_count, 2 * local_columns, width)),
         [SMEM, VMEM],
     )
-    order = step_order(chip_count)
+    order = step_order(chip_count, PROJ_STEPS)
     moved = {0: given[0]}
     for step in order:
         moved[step] = swap(given[step], 2 * step)
     fine = fine_source.reshape(plane_count, local_columns, 2 * comp_count, rhs_count)
     halves = fine.reshape((chip_count, 2) + fine.shape[1:])
     other = swap(lax.dynamic_index_in_dim(halves, 1 - device % 2, axis=1, keepdims=False), 1)
-    steps = order + [0]
+    steps = step_order(chip_count, SOURCE_STEPS) + [0]
     parts = {}
     for step in steps:
         part = whole_call(
@@ -199,55 +200,74 @@
     )
 
 
-def operator_kernel(count, mass_ref, links_ref, residual_ref, *refs):
-    mapped_ref, sums_ref, packed_ref = refs[-3:]
-    near = packed_ref.shape[0]
-    nearby = refs[:near]
-    basis = refs[near:near + count]
-    site_count, comp_count, _ = links_ref.shape
-    rhs_count = residual_ref.shape[2]
+def pack_vector(vector, packed_ref, number):
+    half = vector.shape[1] // 2
+    rhs_count = vector.shape[2]
+    for site in range(vector.shape[0]):
+        real = vector[site, :half]
+        imag = vector[site, half:]
+        packed_ref[number, site, :half, :rhs_count] = real
+        packed_ref[number, site, :half, rhs_count:] = imag
+        packed_ref[number, site, half:, :rhs_count] = -imag
+        packed_ref[number, site, half:, rhs_count:] = real
+
+
+def stacked(product):
+    rhs_count = product.shape[1] // 2
+    return jnp.concatenate([product[:, :rhs_count], product[:, rhs_count:]], axis=0)
+
+
+def slice_kernel(mass_ref, links_ref, own_ref, mapped_ref, packed_ref):
+    site_count, _, _ = links_ref.shape
     line_count = site_count // LX
     mass = mass_ref[0]
-    for number, vector in enumerate(nearby):
-        for site in range(site_count):
-            real = vector[site, :comp_count]
-            imag = vector[site, comp_count:]
-            packed_ref[number, site, :comp_count, :rhs_count] = real
-            packed_ref[number, site, :comp_count, rhs_count:] = imag
-            packed_ref[number, site, comp_count:, :rhs_count] = -imag
-            packed_ref[number, site, comp_count:, rhs_count:] = real
-    totals = [jnp.zeros((8, rhs_count), jnp.float32) for _ in range(3 + 2 * count)]
+    pack_vector(own_ref, packed_ref, 0)
     for site in range(site_count):
         line, column = divmod(site, LX)
         places = [
-            (0, line, column),
-            (0, line, (column + 1) % LX),
-            (0, line, (column - 1) % LX),
-            (0, (line + 1) % line_count, column),
-            (0, (line - 1) % line_count, column),
-            (1, line, column),
-            (2, line, column),
-            (3, line, column),
-            (near - 1, line, column),
+            (line, column),
+            (line, (column + 1) % LX),
+            (line, (column - 1) % LX),
+            ((line + 1) % line_count, column),
+            ((line - 1) % line_count, column),
         ]
-        right = jnp.concatenate([packed_ref[n, y * LX + x] for n, y, x in places], axis=0)
-        product = jnp.dot(links_ref[site], right, preferred_element_type=jnp.float32)
-        own = nearby[0][site].astype(jnp.float32)
-        mapped = (
-            jnp.concatenate([product[:, :rhs_count], product[:, rhs_count:]], axis=0) + mass * own
-        )
+        right = jnp.concatenate([packed_ref[0, y * LX + x] for y, x in places], axis=0)
+        product = jnp.dot(
+            links_ref[site, :, :right.shape[0]], right, preferred_element_type=jnp.float32
+        )
+        mapped_ref[site] = stacked(product) + mass * own_ref[site].astype(jnp.float32)
+
+
+def remote_kernel(count, near, links_ref, partial_ref, residual_ref, *refs):
+    mapped_ref, sums_ref, packed_ref = refs[-3:]
+    basis = refs[near:near + count]
+    site_count, comp_count, width = links_ref.shape
+    rhs_count = residual_ref.shape[2]
+    for number in range(near):
+        pack_vector(refs[number], packed_ref, number)
+    start = width - 8 * comp_count
+    spare = start % LANES
+    totals = [jnp.zeros((8, rhs_count), jnp.float32) for _ in range(3 + 2 * count)]
+    for site in range(site_count):
+        blocks = [packed_ref[n, site] for n in (0, 1, 2, near - 1)]
+        if spare:
+            blocks.insert(0, jnp.zeros((spare, 2 * rhs_count), jnp.bfloat16))
+        right = jnp.concatenate(blocks, axis=0)
+        product = jnp.dot(
+            links_ref[site, :, start - spare:], right, preferred_element_type=jnp.float32
+        )
+        mapped = partial_ref[site] + stacked(product)
         mapped_ref[site] = mapped
         held = residual_ref[site]
         parts = [fold(mapped * mapped), *cross(mapped, held, comp_count)]
         for earlier in basis:
             parts += cross(earlier[site], mapped, comp_count)
         totals = [total + part for total, part in zip(totals, parts)]
-    sums = jnp.concatenate(
+    sums_ref[...] = jnp.concatenate(
         [jnp.sum(total, axis=0, keepdims=True) for total in totals]
-        + [jnp.zeros((sums_ref.shape[-2] - len(totals), rhs_count), jnp.float32)],
+        + [jnp.zeros((sums_ref.shape[0] - len(totals), rhs_count), jnp.float32)],
         axis=0,
     )
-    sums_ref[...] = sums
 
 
 def scaled(vector, factor_re, factor_im, half):
@@ -413,17 +433,25 @@
     basis_q, basis_p = [], []
     for iteration in range(ITERS):
         last = iteration == ITERS - 1
-        nearby = [rounded, send(rounded, back), send(rounded, ring)]
+        nearby = [send(rounded, back), send(rounded, ring)]
         nearby.append(send(rounded, earlier))
         if plane_count > 2 * LZ:
             nearby.append(send(rounded, later))
-        operands = [quark_mass, links, residual, *nearby, *basis_q]
+        packed = (site_count, width, 2 * rhs_count)
+        partial = whole_call(
+            slice_kernel,
+            full,
+            (quark_mass, links, rounded),
+            [SMEM, VMEM, VMEM],
+            [pltpu.VMEM((1,) + packed, jnp.bfloat16)],
+        )
+        operands = [links, partial, residual, *nearby, *basis_q]
         mapped, sums = whole_call(
-            lambda *refs: operator_kernel(iteration, *refs),
+            lambda *refs: remote_kernel(iteration, len(nearby), *refs),
             (full, shape(-(-(3 + 2 * iteration) // 8) * 8, rhs_count)),
             operands,
-            [SMEM] + [VMEM] * (len(operands) - 1),
-            [pltpu.VMEM((len(nearby), site_count, width, 2 * rhs_count), jnp.bfloat16)],
+            [VMEM] * len(operands),
+            [pltpu.VMEM((len(nearby),) + packed, jnp.bfloat16)],
         )
         parts = gather_sums(sums, plane_count)
         operands = [*parts, mapped, residual, *basis_q, *basis_p]

time: 104 us -> 102 us (0.981)
  starting transfers between devices: 58.8 us -> 55.1 us
  waiting for transfers between devices: 33.5 us -> 35.4 us
    ppermute x42, starting transfers between devices: 58.8 us -> 55.1 us  [send(): return lax.ppermute(value, 'ta', pairs)]
    ppermute x42, waiting for transfers between devices: 33.5 us -> 35.4 us  [send(): return lax.ppermute(value, 'ta', pairs)]
    pallas_call x19 -> x22, Pallas kernels: 8.04 us -> 8.53 us  [whole_call(): pl.pallas_call(body, out_shape=out_shape, in_specs=specs, out_specs=jax.t...]
  transfers between devices with their start and end apart: 42 -> 42, of which waited for: 20 -> 24; matrix products, arithmetic and copies ran while one was open for 0% -> 0% of each run, Pallas kernels for 4% -> 5%
where the time goes in v1:
time: 102 us
  starting transfers between devices  55.1 us (54%)
  waiting for transfers between devices  35.4 us (35%)
  Pallas kernels  8.53 us (8%)
  local copies, waits for them, and re-layouts  1.69 us (2%)
  between operations  1.54 us (2%)
    ppermute x42, starting transfers between devices, send(): return lax.ppermute(value, 'ta', pairs)  55.1 us
    ppermute x42, waiting for transfers between devices, send(): return lax.ppermute(value, 'ta', pairs)  35.4 us
    pallas_call x22, Pallas kernels, whole_call(): pl.pallas_call(body, out_shape=out_shape, in_specs=specs, out_specs=jax.t...  8.53 us
  transfers between devices with their start and end apart: 42, of which 24 were waited for; matrix products, arithmetic and copies ran while one was open for 0% of the time, Pallas kernels for 5%

profile of v1, /device:TPU:0, one launch (start us, length us, event | category | flops | bytes accessed | tf_op | source)
XLA Modules:
  0.0 102.3 jit_solution(9713537188682707678)
XLA Ops:
  0.7 1.7 %dynamic-slice_bitcast_fusion = bf16[8,8,96,128]{3,2,1,0:T(8,128)(2,1)S(1)} fusion(bf16[8,2,8,96,128]{4,3,2,1,0:T(8,128)(2,1)} %bitcast.11, s32[]{:T(128)S(6)} %select_n.12), kind=kLoop, calls=%fused_computation | loop fusion | bytes 3145732 | tf_op jit(solution)/shard_map/jit(dynamic_index_in_dim)/squeeze | solution.py:140
  3.0 4.7 %collective-permute-start = (bf16[16,2304]{1,0:T(8,128)(2,1)S(1)}, bf16[16,2304]{1,0:T(8,128)(2,1)S(1)}, u32[]{:S(2)}, u32[]{:S(2)}) collective-permute-start(bf16[16,2304]{1,0:T(8,128)(2,1)S(1)} %get-tuple-element.32), channel_id=1, source_target_pairs={{0,12},{1,13},{2,14},{3,15},{4,8},{5,9},{6,10},{7,11},{8,4},{9,5},... | collective-permute-start | bytes 221192 | tf_op jit(solution)/shard_map/ppermute | solution.py:23
  10.8 2.6 %collective-permute-start.7 = (bf16[16,2304]{1,0:T(8,128)(2,1)S(1)}, bf16[16,2304]{1,0:T(8,128)(2,1)S(1)}, u32[]{:S(2)}, u32[]{:S(2)}) collective-permute-start(bf16[16,2304]{1,0:T(8,128)(2,1)S(1)} %get-tuple-element.35), channel_id=1, source_target_pairs={{0,10},{1,11},{2,8},{3,9},{4,14},{5,15},{6,12},{7,13},{8,2},{9,3},... | collective-permute-start | bytes 221192 | tf_op jit(solution)/shard_map/ppermute | solution.py:23
  13.4 1.3 %collective-permute-done.3.refs_1_ = bf16[16,2304]{1,0:T(8,128)(2,1)S(1)} collective-permute-done((bf16[16,2304]{1,0:T(8,128)(2,1)S(1)}, bf16[16,2304]{1,0:T(8,128)(2,1)S(1)}, u32[]{:S(2)}, u32[]{:S(2)}) %collective-permute-start.3) | collective-permute-done | bytes 73760 | tf_op jit(solution)/shard_map/ppermute | solution.py:23
  14.9 2.0 %collective-permute-start.11 = (bf16[16,2304]{1,0:T(8,128)(2,1)S(1)}, bf16[16,2304]{1,0:T(8,128)(2,1)S(1)}, u32[]{:S(2)}, u32[]{:S(2)}) collective-permute-start(bf16[16,2304]{1,0:T(8,128)(2,1)S(1)} %get-tuple-element.37), channel_id=1, source_target_pairs={{0,2},{1,3},{2,0},{3,1},{4,6},{5,7},{6,4},{7,5},{8,10},{9,11},{10,... | collective-permute-start | bytes 221192 | tf_op jit(solution)/shard_map/ppermute | solution.py:23
  17.9 2.1 %collective-permute-start.2 = (f32[96,128]{1,0:T(8,128)S(1)}, f32[96,128]{1,0:T(8,128)S(1)}, u32[]{:S(2)}, u32[]{:S(2)}) collective-permute-start(f32[96,128]{1,0:T(8,128)S(1)} %shard_map.60), channel_id=1, source_target_pairs={{0,12},{1,13},{2,14},{3,15},{4,8},{5,9},{6,10},{7,11},{8,4},{9,5},... | collective-permute-start | bytes 147464 | tf_op jit(solution)/shard_map/ppermute | solution.py:23
  22.1 3.1 %collective-permute-start.6 = (f32[96,128]{1,0:T(8,128)S(1)}, f32[96,128]{1,0:T(8,128)S(1)}, u32[]{:S(2)}, u32[]{:S(2)}) collective-permute-start(f32[96,128]{1,0:T(8,128)S(1)} %shard_map.62), channel_id=1, source_target_pairs={{0,14},{1,15},{2,12},{3,13},{4,10},{5,11},{6,8},{7,9},{8,6},{9,7},... | collective-permute-start | bytes 147464 | tf_op jit(solution)/shard_map/ppermute | solution.py:23
  27.4 2.4 %collective-permute-start.10 = (f32[96,128]{1,0:T(8,128)S(1)}, f32[96,128]{1,0:T(8,128)S(1)}, u32[]{:S(2)}, u32[]{:S(2)}) collective-permute-start(f32[96,128]{1,0:T(8,128)S(1)} %shard_map.64), channel_id=1, source_target_pairs={{0,8},{1,9},{2,10},{3,11},{4,12},{5,13},{6,14},{7,15},{8,0},{9,1},... | collective-permute-start | bytes 147464 | tf_op jit(solution)/shard_map/ppermute | solution.py:23
  32.4 2.0 %collective-permute-done.12.refs_6_ = f32[96,128]{1,0:T(8,128)S(1)} collective-permute-done((f32[96,128]{1,0:T(8,128)S(1)}, f32[96,128]{1,0:T(8,128)S(1)}, u32[]{:S(2)}, u32[]{:S(2)}) %collective-permute-start.12) | collective-permute-done | bytes 49184 | tf_op jit(solution)/shard_map/ppermute | solution.py:23
  36.1 2.6 %collective-permute-start.15 = (bf16[8,96,128]{2,1,0:T(8,128)(2,1)S(1)}, bf16[8,96,128]{2,1,0:T(8,128)(2,1)S(1)}, u32[]{:S(2)}, u32[]{:S(2)}) collective-permute-start(bf16[8,96,128]{2,1,0:T(8,128)(2,1)S(1)} %get-tuple-element.40.own_ref), channel_id=1, source_target_pairs={{1,0},{2,1},{3,2},{4,3},{5,4},{6,5},{7,6},{0,7},{9,8},{10,9},{11,1... | collective-permute-start | bytes 589832 | tf_op jit(solution)/shard_map/ppermute | solution.py:23
  39.9 3.9 %collective-permute-done.17.refs_5_ = bf16[8,96,128]{2,1,0:T(8,128)(2,1)S(1)} collective-permute-done((bf16[8,96,128]{2,1,0:T(8,128)(2,1)S(1)}, bf16[8,96,128]{2,1,0:T(8,128)(2,1)S(1)}, u32[]{:S(2)}, u32[]{:S(2)}) %collective-permute-start.17) | collective-permute-done | bytes 196640 | tf_op jit(solution)/shard_map/ppermute | solution.py:23
  44.3 2.1 %collective-permute-start.20 = (f32[8,128]{1,0:T(8,128)S(1)}, f32[8,128]{1,0:T(8,128)S(1)}, u32[]{:S(2)}, u32[]{:S(2)}) collective-permute-start(f32[8,128]{1,0:T(8,128)S(1)} %get-tuple-element.42.refs_0_), channel_id=1, source_target_pairs={{0,12},{1,13},{2,14},{3,15},{4,8},{5,9},{6,10},{7,11},{8,4},{9,5},... | collective-permute-start | bytes 12296 | tf_op jit(solution)/shard_map/ppermute | solution.py:23
  47.4 1.4 %collective-permute-start.18 = (f32[8,128]{1,0:T(8,128)S(1)}, f32[8,128]{1,0:T(8,128)S(1)}, u32[]{:S(2)}, u32[]{:S(2)}) collective-permute-start(f32[8,128]{1,0:T(8,128)S(1)} %get-tuple-element.42.refs_0_), channel_id=1, source_target_pairs={{0,4},{1,5},{2,6},{3,7},{4,0},{5,1},{6,2},{7,3},{8,12},{9,13},{10,... | collective-permute-start | bytes 12296 | tf_op jit(solution)/shard_map/ppermute | solution.py:23
  51.0 1.4 %collective-permute-start.23 = (f32[8,128]{1,0:T(8,128)S(1)}, f32[8,128]{1,0:T(8,128)S(1)}, u32[]{:S(2)}, u32[]{:S(2)}) collective-permute-start(f32[8,128]{1,0:T(8,128)S(1)} %shard_map.71.refs_0_), channel_id=1, source_target_pairs={{0,3},{1,2},{2,1},{3,0},{4,7},{5,6},{6,5},{7,4},{8,11},{9,10},{10,... | collective-permute-start | bytes 12296 | tf_op jit(solution)/shard_map/ppermute | solution.py:23
  54.0 2.0 %collective-permute-done.22.refs_2_ = f32[8,128]{1,0:T(8,128)S(1)} collective-permute-done((f32[8,128]{1,0:T(8,128)S(1)}, f32[8,128]{1,0:T(8,128)S(1)}, u32[]{:S(2)}, u32[]{:S(2)}) %collective-permute-start.22) | collective-permute-done | bytes 4128 | tf_op jit(solution)/shard_map/ppermute | solution.py:23
  56.2 1.7 %collective-permute-start.26 = (bf16[8,96,128]{2,1,0:T(8,128)(2,1)S(1)}, bf16[8,96,128]{2,1,0:T(8,128)(2,1)S(1)}, u32[]{:S(2)}, u32[]{:S(2)}) collective-permute-start(bf16[8,96,128]{2,1,0:T(8,128)(2,1)S(1)} %get-tuple-element.44.own_ref), channel_id=1, source_target_pairs={{8,0},{9,1},{10,2},{11,3},{12,4},{13,5},{14,6},{15,7},{0,8},{1,9},... | collective-permute-start | bytes 589832 | tf_op jit(solution)/shard_map/ppermute | solution.py:23
  58.0 2.6 %collective-permute-start.24 = (bf16[8,96,128]{2,1,0:T(8,128)(2,1)S(1)}, bf16[8,96,128]{2,1,0:T(8,128)(2,1)S(1)}, u32[]{:S(2)}, u32[]{:S(2)}) collective-permute-start(bf16[8,96,128]{2,1,0:T(8,128)(2,1)S(1)} %get-tuple-element.44.own_ref), channel_id=1, source_target_pairs={{1,0},{2,1},{3,2},{4,3},{5,4},{6,5},{7,6},{0,7},{9,8},{10,9},{11,1... | collective-permute-start | bytes 589832 | tf_op jit(solution)/shard_map/ppermute | solution.py:23
  61.1 5.7 %collective-permute-done.26.refs_5_ = bf16[8,96,128]{2,1,0:T(8,128)(2,1)S(1)} collective-permute-done((bf16[8,96,128]{2,1,0:T(8,128)(2,1)S(1)}, bf16[8,96,128]{2,1,0:T(8,128)(2,1)S(1)}, u32[]{:S(2)}, u32[]{:S(2)}) %collective-permute-start.26) | collective-permute-done | bytes 196640 | tf_op jit(solution)/shard_map/ppermute | solution.py:23
  69.7 2.8 %collective-permute-start.27 = (f32[8,128]{1,0:T(8,128)S(1)}, f32[8,128]{1,0:T(8,128)S(1)}, u32[]{:S(2)}, u32[]{:S(2)}) collective-permute-start(f32[8,128]{1,0:T(8,128)S(1)} %get-tuple-element.47.refs_0_), channel_id=1, source_target_pairs={{0,4},{1,5},{2,6},{3,7},{4,0},{5,1},{6,2},{7,3},{8,12},{9,13},{10,... | collective-permute-start | bytes 12296 | tf_op jit(solution)/shard_map/ppermute | solution.py:23
  78.7 2.0 %collective-permute-start.35 = (bf16[8,96,128]{2,1,0:T(8,128)(2,1)S(1)}, bf16[8,96,128]{2,1,0:T(8,128)(2,1)S(1)}, u32[]{:S(2)}, u32[]{:S(2)}) collective-permute-start(bf16[8,96,128]{2,1,0:T(8,128)(2,1)S(1)} %get-tuple-element.52.own_ref), channel_id=1, source_target_pairs={{8,0},{9,1},{10,2},{11,3},{12,4},{13,5},{14,6},{15,7},{0,8},{1,9},... | collective-permute-start | bytes 589832 | tf_op jit(solution)/shard_map/ppermute | solution.py:23
  80.7 2.6 %collective-permute-start.33 = (bf16[8,96,128]{2,1,0:T(8,128)(2,1)S(1)}, bf16[8,96,128]{2,1,0:T(8,128)(2,1)S(1)}, u32[]{:S(2)}, u32[]{:S(2)}) collective-permute-start(bf16[8,96,128]{2,1,0:T(8,128)(2,1)S(1)} %get-tuple-element.52.own_ref), channel_id=1, source_target_pairs={{1,0},{2,1},{3,2},{4,3},{5,4},{6,5},{7,6},{0,7},{9,8},{10,9},{11,1... | collective-permute-start | bytes 589832 | tf_op jit(solution)/shard_map/ppermute | solution.py:23
  83.8 6.2 %collective-permute-done.35.refs_5_ = bf16[8,96,128]{2,1,0:T(8,128)(2,1)S(1)} collective-permute-done((bf16[8,96,128]{2,1,0:T(8,128)(2,1)S(1)}, bf16[8,96,128]{2,1,0:T(8,128)(2,1)S(1)}, u32[]{:S(2)}, u32[]{:S(2)}) %collective-permute-start.35) | collective-permute-done | bytes 196640 | tf_op jit(solution)/shard_map/ppermute | solution.py:23
  90.5 2.1 %collective-permute-start.38 = (f32[8,128]{1,0:T(8,128)S(1)}, f32[8,128]{1,0:T(8,128)S(1)}, u32[]{:S(2)}, u32[]{:S(2)}) collective-permute-start(f32[8,128]{1,0:T(8,128)S(1)} %get-tuple-element.55.refs_0_), channel_id=1, source_target_pairs={{0,12},{1,13},{2,14},{3,15},{4,8},{5,9},{6,10},{7,11},{8,4},{9,5},... | collective-permute-start | bytes 12296 | tf_op jit(solution)/shard_map/ppermute | solution.py:23
  92.7 2.3 %collective-permute-start.36 = (f32[8,128]{1,0:T(8,128)S(1)}, f32[8,128]{1,0:T(8,128)S(1)}, u32[]{:S(2)}, u32[]{:S(2)}) collective-permute-start(f32[8,128]{1,0:T(8,128)S(1)} %get-tuple-element.55.refs_0_), channel_id=1, source_target_pairs={{0,4},{1,5},{2,6},{3,7},{4,0},{5,1},{6,2},{7,3},{8,12},{9,13},{10,... | collective-permute-start | bytes 12296 | tf_op jit(solution)/shard_map/ppermute | solution.py:23
  (89 shorter events, 37.2 us)
Async XLA Ops:
  2.3 12.6 %collective-permute-start.1 = (bf16[8,8,96,128]{3,2,1,0:T(8,128)(2,1)S(1)}, bf16[8,8,96,128]{3,2,1,0:T(8,128)(2,1)S(1)}, u32[]{:S(2)}, u32[]{:S(2)}) collective-permute-start(bf16[8,8,96,128]{3,2,1,0:T(8,128)(2,1)S(1)} %dynamic-slice_bitcast_fusion), channel_id=1, source_target_pairs={{0,1},{1,0},{2,3},{3,2},{4,5},{5,4},{6,7},{7,6},{8,9},{9,8},{10,11... | collective-permute-start | bytes 4718600 | tf_op jit(solution)/shard_map/ppermute | solution.py:23
  3.0 7.9 %collective-permute-start = (bf16[16,2304]{1,0:T(8,128)(2,1)S(1)}, bf16[16,2304]{1,0:T(8,128)(2,1)S(1)}, u32[]{:S(2)}, u32[]{:S(2)}) collective-permute-start(bf16[16,2304]{1,0:T(8,128)(2,1)S(1)} %get-tuple-element.32), channel_id=1, source_target_pairs={{0,12},{1,13},{2,14},{3,15},{4,8},{5,9},{6,10},{7,11},{8,4},{9,5},... | collective-permute-start | bytes 221192 | tf_op jit(solution)/shard_map/ppermute | solution.py:23
  7.6 7.1 %collective-permute-start.3 = (bf16[16,2304]{1,0:T(8,128)(2,1)S(1)}, bf16[16,2304]{1,0:T(8,128)(2,1)S(1)}, u32[]{:S(2)}, u32[]{:S(2)}) collective-permute-start(bf16[16,2304]{1,0:T(8,128)(2,1)S(1)} %get-tuple-element.33), channel_id=1, source_target_pairs={{0,6},{1,7},{2,4},{3,5},{4,2},{5,3},{6,0},{7,1},{8,14},{9,15},{10,... | collective-permute-start | bytes 221192 | tf_op jit(solution)/shard_map/ppermute | solution.py:23
  8.1 9.7 %collective-permute-start.5 = (bf16[16,2304]{1,0:T(8,128)(2,1)S(1)}, bf16[16,2304]{1,0:T(8,128)(2,1)S(1)}, u32[]{:S(2)}, u32[]{:S(2)}) collective-permute-start(bf16[16,2304]{1,0:T(8,128)(2,1)S(1)} %get-tuple-element.34), channel_id=1, source_target_pairs={{0,14},{1,15},{2,12},{3,13},{4,10},{5,11},{6,8},{7,9},{8,6},{9,7},... | collective-permute-start | bytes 221192 | tf_op jit(solution)/shard_map/ppermute | solution.py:23
  9.4 10.6 %collective-permute-start.13 = (bf16[16,2304]{1,0:T(8,128)(2,1)S(1)}, bf16[16,2304]{1,0:T(8,128)(2,1)S(1)}, u32[]{:S(2)}, u32[]{:S(2)}) collective-permute-start(bf16[16,2304]{1,0:T(8,128)(2,1)S(1)} %get-tuple-element.38), channel_id=1, source_target_pairs={{0,4},{1,5},{2,6},{3,7},{4,0},{5,1},{6,2},{7,3},{8,12},{9,13},{10,... | collective-permute-start | bytes 221192 | tf_op jit(solution)/shard_map/ppermute | solution.py:23
  10.8 11.3 %collective-permute-start.7 = (bf16[16,2304]{1,0:T(8,128)(2,1)S(1)}, bf16[16,2304]{1,0:T(8,128)(2,1)S(1)}, u32[]{:S(2)}, u32[]{:S(2)}) collective-permute-start(bf16[16,2304]{1,0:T(8,128)(2,1)S(1)} %get-tuple-element.35), channel_id=1, source_target_pairs={{0,10},{1,11},{2,8},{3,9},{4,14},{5,15},{6,12},{7,13},{8,2},{9,3},... | collective-permute-start | bytes 221192 | tf_op jit(solution)/shard_map/ppermute | solution.py:23
  14.8 10.9 %collective-permute-start.9 = (bf16[16,2304]{1,0:T(8,128)(2,1)S(1)}, bf16[16,2304]{1,0:T(8,128)(2,1)S(1)}, u32[]{:S(2)}, u32[]{:S(2)}) collective-permute-start(bf16[16,2304]{1,0:T(8,128)(2,1)S(1)} %get-tuple-element.36), channel_id=1, source_target_pairs={{0,8},{1,9},{2,10},{3,11},{4,12},{5,13},{6,14},{7,15},{8,0},{9,1},... | collective-permute-start | bytes 221192 | tf_op jit(solution)/shard_map/ppermute | solution.py:23
  14.9 12.4 %collective-permute-start.11 = (bf16[16,2304]{1,0:T(8,128)(2,1)S(1)}, bf16[16,2304]{1,0:T(8,128)(2,1)S(1)}, u32[]{:S(2)}, u32[]{:S(2)}) collective-permute-start(bf16[16,2304]{1,0:T(8,128)(2,1)S(1)} %get-tuple-element.37), channel_id=1, source_target_pairs={{0,2},{1,3},{2,0},{3,1},{4,6},{5,7},{6,4},{7,5},{8,10},{9,11},{10,... | collective-permute-start | bytes 221192 | tf_op jit(solution)/shard_map/ppermute | solution.py:23
  17.9 12.4 %collective-permute-start.2 = (f32[96,128]{1,0:T(8,128)S(1)}, f32[96,128]{1,0:T(8,128)S(1)}, u32[]{:S(2)}, u32[]{:S(2)}) collective-permute-start(f32[96,128]{1,0:T(8,128)S(1)} %shard_map.60), channel_id=1, source_target_pairs={{0,12},{1,13},{2,14},{3,15},{4,8},{5,9},{6,10},{7,11},{8,4},{9,5},... | collective-permute-start | bytes 147464 | tf_op jit(solution)/shard_map/ppermute | solution.py:23
  20.0 11.2 %collective-permute-start.4 = (f32[96,128]{1,0:T(8,128)S(1)}, f32[96,128]{1,0:T(8,128)S(1)}, u32[]{:S(2)}, u32[]{:S(2)}) collective-permute-start(f32[96,128]{1,0:T(8,128)S(1)} %shard_map.61), channel_id=1, source_target_pairs={{0,6},{1,7},{2,4},{3,5},{4,2},{5,3},{6,0},{7,1},{8,14},{9,15},{10,... | collective-permute-start | bytes 147464 | tf_op jit(solution)/shard_map/ppermute | solution.py:23
  22.1 9.6 %collective-permute-start.6 = (f32[96,128]{1,0:T(8,128)S(1)}, f32[96,128]{1,0:T(8,128)S(1)}, u32[]{:S(2)}, u32[]{:S(2)}) collective-permute-start(f32[96,128]{1,0:T(8,128)S(1)} %shard_map.62), channel_id=1, source_target_pairs={{0,14},{1,15},{2,12},{3,13},{4,10},{5,11},{6,8},{7,9},{8,6},{9,7},... | collective-permute-start | bytes 147464 | tf_op jit(solution)/shard_map/ppermute | solution.py:23
  25.7 6.1 %collective-permute-start.8 = (f32[96,128]{1,0:T(8,128)S(1)}, f32[96,128]{1,0:T(8,128)S(1)}, u32[]{:S(2)}, u32[]{:S(2)}) collective-permute-start(f32[96,128]{1,0:T(8,128)S(1)} %shard_map.63), channel_id=1, source_target_pairs={{0,10},{1,11},{2,8},{3,9},{4,14},{5,15},{6,12},{7,13},{8,2},{9,3},... | collective-permute-start | bytes 147464 | tf_op jit(solution)/shard_map/ppermute | solution.py:23
  35.4 8.4 %collective-permute-start.17 = (bf16[8,96,128]{2,1,0:T(8,128)(2,1)S(1)}, bf16[8,96,128]{2,1,0:T(8,128)(2,1)S(1)}, u32[]{:S(2)}, u32[]{:S(2)}) collective-permute-start(bf16[8,96,128]{2,1,0:T(8,128)(2,1)S(1)} %get-tuple-element.40.own_ref), channel_id=1, source_target_pairs={{8,0},{9,1},{10,2},{11,3},{12,4},{13,5},{14,6},{15,7},{0,8},{1,9},... | collective-permute-start | bytes 589832 | tf_op jit(solution)/shard_map/ppermute | solution.py:23
  36.1 7.7 %collective-permute-start.16 = (bf16[8,96,128]{2,1,0:T(8,128)(2,1)S(1)}, bf16[8,96,128]{2,1,0:T(8,128)(2,1)S(1)}, u32[]{:S(2)}, u32[]{:S(2)}) collective-permute-start(bf16[8,96,128]{2,1,0:T(8,128)(2,1)S(1)} %get-tuple-element.40.own_ref), channel_id=1, source_target_pairs={{0,1},{1,2},{2,3},{3,4},{4,5},{5,6},{6,7},{7,0},{8,9},{9,10},{10,1... | collective-permute-start | bytes 589832 | tf_op jit(solution)/shard_map/ppermute | solution.py:23
  36.1 7.7 %collective-permute-start.15 = (bf16[8,96,128]{2,1,0:T(8,128)(2,1)S(1)}, bf16[8,96,128]{2,1,0:T(8,128)(2,1)S(1)}, u32[]{:S(2)}, u32[]{:S(2)}) collective-permute-start(bf16[8,96,128]{2,1,0:T(8,128)(2,1)S(1)} %get-tuple-element.40.own_ref), channel_id=1, source_target_pairs={{1,0},{2,1},{3,2},{4,3},{5,4},{6,5},{7,6},{0,7},{9,8},{10,9},{11,1... | collective-permute-start | bytes 589832 | tf_op jit(solution)/shard_map/ppermute | solution.py:23
  44.3 5.5 %collective-permute-start.20 = (f32[8,128]{1,0:T(8,128)S(1)}, f32[8,128]{1,0:T(8,128)S(1)}, u32[]{:S(2)}, u32[]{:S(2)}) collective-permute-start(f32[8,128]{1,0:T(8,128)S(1)} %get-tuple-element.42.refs_0_), channel_id=1, source_target_pairs={{0,12},{1,13},{2,14},{3,15},{4,8},{5,9},{6,10},{7,11},{8,4},{9,5},... | collective-permute-start | bytes 12296 | tf_op jit(solution)/shard_map/ppermute | solution.py:23
  56.2 10.5 %collective-permute-start.26 = (bf16[8,96,128]{2,1,0:T(8,128)(2,1)S(1)}, bf16[8,96,128]{2,1,0:T(8,128)(2,1)S(1)}, u32[]{:S(2)}, u32[]{:S(2)}) collective-permute-start(bf16[8,96,128]{2,1,0:T(8,128)(2,1)S(1)} %get-tuple-element.44.own_ref), channel_id=1, source_target_pairs={{8,0},{9,1},{10,2},{11,3},{12,4},{13,5},{14,6},{15,7},{0,8},{1,9},... | collective-permute-start | bytes 589832 | tf_op jit(solution)/shard_map/ppermute | solution.py:23
  58.0 9.6 %collective-permute-start.25 = (bf16[8,96,128]{2,1,0:T(8,128)(2,1)S(1)}, bf16[8,96,128]{2,1,0:T(8,128)(2,1)S(1)}, u32[]{:S(2)}, u32[]{:S(2)}) collective-permute-start(bf16[8,96,128]{2,1,0:T(8,128)(2,1)S(1)} %get-tuple-element.44.own_ref), channel_id=1, source_target_pairs={{0,1},{1,2},{2,3},{3,4},{4,5},{5,6},{6,7},{7,0},{8,9},{9,10},{10,1... | collective-permute-start | bytes 589832 | tf_op jit(solution)/shard_map/ppermute | solution.py:23
  58.0 9.6 %collective-permute-start.24 = (bf16[8,96,128]{2,1,0:T(8,128)(2,1)S(1)}, bf16[8,96,128]{2,1,0:T(8,128)(2,1)S(1)}, u32[]{:S(2)}, u32[]{:S(2)}) collective-permute-start(bf16[8,96,128]{2,1,0:T(8,128)(2,1)S(1)} %get-tuple-element.44.own_ref), channel_id=1, source_target_pairs={{1,0},{2,1},{3,2},{4,3},{5,4},{6,5},{7,6},{0,7},{9,8},{10,9},{11,1... | collective-permute-start | bytes 589832 | tf_op jit(solution)/shard_map/ppermute | solution.py:23
  68.1 5.5 %collective-permute-start.29 = (f32[8,128]{1,0:T(8,128)S(1)}, f32[8,128]{1,0:T(8,128)S(1)}, u32[]{:S(2)}, u32[]{:S(2)}) collective-permute-start(f32[8,128]{1,0:T(8,128)S(1)} %get-tuple-element.47.refs_0_), channel_id=1, source_target_pairs={{0,12},{1,13},{2,14},{3,15},{4,8},{5,9},{6,10},{7,11},{8,4},{9,5},... | collective-permute-start | bytes 12296 | tf_op jit(solution)/shard_map/ppermute | solution.py:23
  78.7 11.3 %collective-permute-start.35 = (bf16[8,96,128]{2,1,0:T(8,128)(2,1)S(1)}, bf16[8,96,128]{2,1,0:T(8,128)(2,1)S(1)}, u32[]{:S(2)}, u32[]{:S(2)}) collective-permute-start(bf16[8,96,128]{2,1,0:T(8,128)(2,1)S(1)} %get-tuple-element.52.own_ref), channel_id=1, source_target_pairs={{8,0},{9,1},{10,2},{11,3},{12,4},{13,5},{14,6},{15,7},{0,8},{1,9},... | collective-permute-start | bytes 589832 | tf_op jit(solution)/shard_map/ppermute | solution.py:23
  80.7 9.3 %collective-permute-start.34 = (bf16[8,96,128]{2,1,0:T(8,128)(2,1)S(1)}, bf16[8,96,128]{2,1,0:T(8,128)(2,1)S(1)}, u32[]{:S(2)}, u32[]{:S(2)}) collective-permute-start(bf16[8,96,128]{2,1,0:T(8,128)(2,1)S(1)} %get-tuple-element.52.own_ref), channel_id=1, source_target_pairs={{0,1},{1,2},{2,3},{3,4},{4,5},{5,6},{6,7},{7,0},{8,9},{9,10},{10,1... | collective-permute-start | bytes 589832 | tf_op jit(solution)/shard_map/ppermute | solution.py:23
  80.7 9.3 %collective-permute-start.33 = (bf16[8,96,128]{2,1,0:T(8,128)(2,1)S(1)}, bf16[8,96,128]{2,1,0:T(8,128)(2,1)S(1)}, u32[]{:S(2)}, u32[]{:S(2)}) collective-permute-start(bf16[8,96,128]{2,1,0:T(8,128)(2,1)S(1)} %get-tuple-element.52.own_ref), channel_id=1, source_target_pairs={{1,0},{2,1},{3,2},{4,3},{5,4},{6,5},{7,6},{0,7},{9,8},{10,9},{11,1... | collective-permute-start | bytes 589832 | tf_op jit(solution)/shard_map/ppermute | solution.py:23
  90.5 5.5 %collective-permute-start.38 = (f32[8,128]{1,0:T(8,128)S(1)}, f32[8,128]{1,0:T(8,128)S(1)}, u32[]{:S(2)}, u32[]{:S(2)}) collective-permute-start(f32[8,128]{1,0:T(8,128)S(1)} %get-tuple-element.55.refs_0_), channel_id=1, source_target_pairs={{0,12},{1,13},{2,14},{3,15},{4,8},{5,9},{6,10},{7,11},{8,4},{9,5},... | collective-permute-start | bytes 12296 | tf_op jit(solution)/shard_map/ppermute | solution.py:23
  (21 other events, 95.3 us)

commit v2 on v1

--- a/solution.py
+++ b/solution.py
@@ -105,8 +105,14 @@
     source_ref[pair_count:] = total[:, rhs_count:]
 
 
+def round_kernel(*refs):
+    for number, part in enumerate(refs[:-1]):
+        refs[-1][number] = part[...].astype(jnp.bfloat16)
+
+
 def join_kernel(steps, device_ref, *refs):
-    parts, (source_ref, rounded_ref) = refs[:-2], refs[-2:]
+    parts, (source_ref, rounded_ref, late_ref) = refs[:-3], refs[-3:]
+    round_kernel(*parts[len(parts) - late_ref.shape[0]:], late_ref)
     chip = device_ref[0] // 2
     for step, part in zip(steps, parts):
         source_ref[chip ^ step] = part[...]
@@ -150,12 +156,18 @@
         )
         parts[step] = swap(part, 2 * step) if step else part
     shape = (chip_count, 2 * comp_count, rhs_count)
-    return whole_call(
+    half = jax.ShapeDtypeStruct((chip_count // 2,) + shape[1:], low)
+    pieces = [steps[:chip_count // 2], steps[chip_count // 2:]]
+    first = whole_call(
+        round_kernel, half, [parts[step] for step in pieces[0]], [VMEM] * (chip_count // 2)
+    )
+    source, rounded, second = whole_call(
         lambda *refs: join_kernel(steps, *refs),
-        (jax.ShapeDtypeStruct(shape, jnp.float32), jax.ShapeDtypeStruct(shape, low)),
+        (jax.ShapeDtypeStruct(shape, jnp.float32), jax.ShapeDtypeStruct(shape, low), half),
         (place, *(parts[step] for step in steps)),
         [SMEM] + [VMEM] * chip_count,
     )
+    return source, rounded, pieces, (first, second)
 
 
 def real_weights(proj_view):
@@ -200,12 +212,12 @@
     )
 
 
-def pack_vector(vector, packed_ref, number):
+def pack_vector(vector, packed_ref, number, sites=None):
     half = vector.shape[1] // 2
     rhs_count = vector.shape[2]
-    for site in range(vector.shape[0]):
-        real = vector[site, :half]
-        imag = vector[site, half:]
+    for index, site in enumerate(sites or range(vector.shape[0])):
+        real = vector[index, :half]
+        imag = vector[index, half:]
         packed_ref[number, site, :half, :rhs_count] = real
         packed_ref[number, site, :half, rhs_count:] = imag
         packed_ref[number, site, half:, :rhs_count] = -imag
@@ -238,13 +250,22 @@
         mapped_ref[site] = stacked(product) + mass * own_ref[site].astype(jnp.float32)
 
 
-def remote_kernel(count, near, links_ref, partial_ref, residual_ref, *refs):
+def remote_kernel(count, near, pieces, device_ref, links_ref, partial_ref, residual_ref, *refs):
     mapped_ref, sums_ref, packed_ref = refs[-3:]
-    basis = refs[near:near + count]
+    vectors = len(refs) - 3 - count
+    basis = refs[vectors:vectors + count]
     site_count, comp_count, width = links_ref.shape
     rhs_count = residual_ref.shape[2]
-    for number in range(near):
-        pack_vector(refs[number], packed_ref, number)
+    parity = device_ref[0] % 2
+    for number in range(2):
+        pack_vector(refs[number], packed_ref, (parity, 1 - parity)[number])
+    if pieces:
+        partner = (device_ref[0] + LZ) % (2 * LZ) // 2
+        for number, steps in enumerate(pieces):
+            pack_vector(refs[2 + number], packed_ref, 2, [partner ^ step for step in steps])
+    else:
+        for number in range(2, near):
+            pack_vector(refs[number], packed_ref, number)
     start = width - 8 * comp_count
     spare = start % LANES
     totals = [jnp.zeros((8, rhs_count), jnp.float32) for _ in range(3 + 2 * count)]
@@ -408,17 +429,21 @@
     chip_count = plane_count // 2
     paired = local_columns * 2 == block_count and local_columns % 8 == 0
     if paired and chip_count & (chip_count - 1) == 0:
-        source, rounded = paired_restriction(fine_source, projectors, comp_count)
+        source, rounded, pieces, halves = paired_restriction(fine_source, projectors, comp_count)
     else:
         source = general_restriction(
             fine_source, projectors, comp_count, site_count, block_count
         )
         rounded = source.astype(jnp.bfloat16)
+        pieces = None
+    if plane_count != 2 * LZ:
+        pieces = None
     links = stencil_links[0]
-    ring = [
-        (plane, plane // LZ * LZ + (plane + 1) % LZ) for plane in range(plane_count)
-    ]
-    back = [(target, origin) for origin, target in ring]
+    inner = [(plane, plane ^ 1) for plane in range(plane_count)]
+    outer = []
+    for plane in range(plane_count):
+        turn = 1 if plane % 2 else -1
+        outer.append((plane, plane // LZ * LZ + (plane + turn) % LZ))
     later = [(plane, (plane + LZ) % plane_count) for plane in range(plane_count)]
     earlier = [(target, origin) for origin, target in later]
 
@@ -428,14 +453,22 @@
     width = 2 * comp_count
     full = shape(site_count, width, rhs_count)
     low = shape(site_count, width, rhs_count, dtype=jnp.bfloat16)
+    device = lax.axis_index("ta").astype(jnp.int32).reshape(1)
     residual = source
     total = None
     basis_q, basis_p = [], []
     for iteration in range(ITERS):
         last = iteration == ITERS - 1
-        nearby = [send(rounded, back), send(rounded, ring)]
-        nearby.append(send(rounded, earlier))
+        nearby = [send(rounded, inner), send(rounded, outer)]
+        parted = pieces if iteration == 0 else None
+        near = 3
+        if parted:
+            nearby.append(send(halves[0], earlier))
+            nearby.append(send(halves[1], earlier))
+        else:
+            nearby.append(send(rounded, earlier))
         if plane_count > 2 * LZ:
+            near = 4
             nearby.append(send(rounded, later))
         packed = (site_count, width, 2 * rhs_count)
         partial = whole_call(
@@ -445,13 +478,13 @@
             [SMEM, VMEM, VMEM],
             [pltpu.VMEM((1,) + packed, jnp.bfloat16)],
         )
-        operands = [links, partial, residual, *nearby, *basis_q]
+        operands = [device, links, partial, residual, *nearby, *basis_q]
         mapped, sums = whole_call(
-            lambda *refs: remote_kernel(iteration, len(nearby), *refs),
+            lambda *refs: remote_kernel(iteration, near, parted, *refs),
             (full, shape(-(-(3 + 2 * iteration) // 8) * 8, rhs_count)),
             operands,
-            [VMEM] * len(operands),
-            [pltpu.VMEM((len(nearby),) + packed, jnp.bfloat16)],
+            [SMEM] + [VMEM] * (len(operands) - 1),
+            [pltpu.VMEM((near,) + packed, jnp.bfloat16)],
         )
         parts = gather_sums(sums, plane_count)
         operands = [*parts, mapped, residual, *basis_q, *basis_p]

time: 102 us -> 107 us (1.049)
  waiting for transfers between devices: 35.4 us -> 40.9 us
  starting transfers between devices: 55.1 us -> 53.6 us
    ppermute x42 -> x43, waiting for transfers between devices: 35.4 us -> 40.9 us  [send(): return lax.ppermute(value, 'ta', pairs)]
    ppermute x42 -> x43, starting transfers between devices: 55.1 us -> 53.6 us  [send(): return lax.ppermute(value, 'ta', pairs)]
    pallas_call x22 -> x23, Pallas kernels: 8.53 us -> 8.82 us  [whole_call(): pl.pallas_call(body, out_shape=out_shape, in_specs=specs, out_specs=jax.t...]
  transfers between devices with their start and end apart: 42 -> 43, of which waited for: 24 -> 22; matrix products, arithmetic and copies ran while one was open for 0% -> 0% of each run, Pallas kernels for 5% -> 5%
where the time goes in v2:
time: 107 us
  starting transfers between devices  53.6 us (50%)
  waiting for transfers between devices  40.9 us (38%)
  Pallas kernels  8.82 us (8%)
  local copies, waits for them, and re-layouts  1.69 us (2%)
  between operations  1.58 us (1%)
    ppermute x43, starting transfers between devices, send(): return lax.ppermute(value, 'ta', pairs)  53.6 us
    ppermute x43, waiting for transfers between devices, send(): return lax.ppermute(value, 'ta', pairs)  40.9 us
    pallas_call x23, Pallas kernels, whole_call(): pl.pallas_call(body, out_shape=out_shape, in_specs=specs, out_specs=jax.t...  8.82 us
  transfers between devices with their start and end apart: 43, of which 22 were waited for; matrix products, arithmetic and copies ran while one was open for 0% of the time, Pallas kernels for 5%

profile of v2, /device:TPU:0, one launch (start us, length us, event | category | flops | bytes accessed | tf_op | source)
XLA Modules:
  0.0 106.6 jit_solution(4566869316540251633)
XLA Ops:
  0.7 1.7 %dynamic-slice_bitcast_fusion = bf16[8,8,96,128]{3,2,1,0:T(8,128)(2,1)S(1)} fusion(bf16[8,2,8,96,128]{4,3,2,1,0:T(8,128)(2,1)} %bitcast.11, s32[]{:T(128)S(6)} %select_n.12), kind=kLoop, calls=%fused_computation | loop fusion | bytes 3145732 | tf_op jit(solution)/shard_map/jit(dynamic_index_in_dim)/squeeze | solution.py:146
  3.0 4.7 %collective-permute-start = (bf16[16,2304]{1,0:T(8,128)(2,1)S(1)}, bf16[16,2304]{1,0:T(8,128)(2,1)S(1)}, u32[]{:S(2)}, u32[]{:S(2)}) collective-permute-start(bf16[16,2304]{1,0:T(8,128)(2,1)S(1)} %get-tuple-element.33), channel_id=1, source_target_pairs={{0,12},{1,13},{2,14},{3,15},{4,8},{5,9},{6,10},{7,11},{8,4},{9,5},... | collective-permute-start | bytes 221192 | tf_op jit(solution)/shard_map/ppermute | solution.py:23
  8.1 1.3 %collective-permute-start.5 = (bf16[16,2304]{1,0:T(8,128)(2,1)S(1)}, bf16[16,2304]{1,0:T(8,128)(2,1)S(1)}, u32[]{:S(2)}, u32[]{:S(2)}) collective-permute-start(bf16[16,2304]{1,0:T(8,128)(2,1)S(1)} %get-tuple-element.35), channel_id=1, source_target_pairs={{0,14},{1,15},{2,12},{3,13},{4,10},{5,11},{6,8},{7,9},{8,6},{9,7},... | collective-permute-start | bytes 221192 | tf_op jit(solution)/shard_map/ppermute | solution.py:23
  10.8 2.6 %collective-permute-start.7 = (bf16[16,2304]{1,0:T(8,128)(2,1)S(1)}, bf16[16,2304]{1,0:T(8,128)(2,1)S(1)}, u32[]{:S(2)}, u32[]{:S(2)}) collective-permute-start(bf16[16,2304]{1,0:T(8,128)(2,1)S(1)} %get-tuple-element.36), channel_id=1, source_target_pairs={{0,10},{1,11},{2,8},{3,9},{4,14},{5,15},{6,12},{7,13},{8,2},{9,3},... | collective-permute-start | bytes 221192 | tf_op jit(solution)/shard_map/ppermute | solution.py:23
  13.4 1.3 %collective-permute-done.3.refs_1_ = bf16[16,2304]{1,0:T(8,128)(2,1)S(1)} collective-permute-done((bf16[16,2304]{1,0:T(8,128)(2,1)S(1)}, bf16[16,2304]{1,0:T(8,128)(2,1)S(1)}, u32[]{:S(2)}, u32[]{:S(2)}) %collective-permute-start.3) | collective-permute-done | bytes 73760 | tf_op jit(solution)/shard_map/ppermute | solution.py:23
  14.9 2.0 %collective-permute-start.11 = (bf16[16,2304]{1,0:T(8,128)(2,1)S(1)}, bf16[16,2304]{1,0:T(8,128)(2,1)S(1)}, u32[]{:S(2)}, u32[]{:S(2)}) collective-permute-start(bf16[16,2304]{1,0:T(8,128)(2,1)S(1)} %get-tuple-element.38), channel_id=1, source_target_pairs={{0,2},{1,3},{2,0},{3,1},{4,6},{5,7},{6,4},{7,5},{8,10},{9,11},{10,... | collective-permute-start | bytes 221192 | tf_op jit(solution)/shard_map/ppermute | solution.py:23
  17.9 2.1 %collective-permute-start.2 = (f32[96,128]{1,0:T(8,128)S(1)}, f32[96,128]{1,0:T(8,128)S(1)}, u32[]{:S(2)}, u32[]{:S(2)}) collective-permute-start(f32[96,128]{1,0:T(8,128)S(1)} %shard_map.60), channel_id=1, source_target_pairs={{0,12},{1,13},{2,14},{3,15},{4,8},{5,9},{6,10},{7,11},{8,4},{9,5},... | collective-permute-start | bytes 147464 | tf_op jit(solution)/shard_map/ppermute | solution.py:23
  22.1 3.1 %collective-permute-start.6 = (f32[96,128]{1,0:T(8,128)S(1)}, f32[96,128]{1,0:T(8,128)S(1)}, u32[]{:S(2)}, u32[]{:S(2)}) collective-permute-start(f32[96,128]{1,0:T(8,128)S(1)} %shard_map.62), channel_id=1, source_target_pairs={{0,14},{1,15},{2,12},{3,13},{4,10},{5,11},{6,8},{7,9},{8,6},{9,7},... | collective-permute-start | bytes 147464 | tf_op jit(solution)/shard_map/ppermute | solution.py:23
  27.4 2.4 %collective-permute-start.10 = (f32[96,128]{1,0:T(8,128)S(1)}, f32[96,128]{1,0:T(8,128)S(1)}, u32[]{:S(2)}, u32[]{:S(2)}) collective-permute-start(f32[96,128]{1,0:T(8,128)S(1)} %shard_map.64), channel_id=1, source_target_pairs={{0,8},{1,9},{2,10},{3,11},{4,12},{5,13},{6,14},{7,15},{8,0},{9,1},... | collective-permute-start | bytes 147464 | tf_op jit(solution)/shard_map/ppermute | solution.py:23
  32.4 2.0 %collective-permute-done.12.refs_6_ = f32[96,128]{1,0:T(8,128)S(1)} collective-permute-done((f32[96,128]{1,0:T(8,128)S(1)}, f32[96,128]{1,0:T(8,128)S(1)}, u32[]{:S(2)}, u32[]{:S(2)}) %collective-permute-start.12) | collective-permute-done | bytes 49184 | tf_op jit(solution)/shard_map/ppermute | solution.py:23
  37.4 2.4 %collective-permute-start.18 = (bf16[4,96,128]{2,1,0:T(8,128)(2,1)S(1)}, bf16[4,96,128]{2,1,0:T(8,128)(2,1)S(1)}, u32[]{:S(2)}, u32[]{:S(2)}) collective-permute-start(bf16[4,96,128]{2,1,0:T(8,128)(2,1)S(1)} %get-tuple-element.43), channel_id=1, source_target_pairs={{8,0},{9,1},{10,2},{11,3},{12,4},{13,5},{14,6},{15,7},{0,8},{1,9},... | collective-permute-start | bytes 294920 | tf_op jit(solution)/shard_map/ppermute | solution.py:23
  40.9 5.9 %collective-permute-done.17.refs_6_ = bf16[4,96,128]{2,1,0:T(8,128)(2,1)S(1)} collective-permute-done((bf16[4,96,128]{2,1,0:T(8,128)(2,1)S(1)}, bf16[4,96,128]{2,1,0:T(8,128)(2,1)S(1)}, u32[]{:S(2)}, u32[]{:S(2)}) %collective-permute-start.17) | collective-permute-done | bytes 98336 | tf_op jit(solution)/shard_map/ppermute | solution.py:23
  46.8 1.6 %collective-permute-done.18.refs_7_ = bf16[4,96,128]{2,1,0:T(8,128)(2,1)S(1)} collective-permute-done((bf16[4,96,128]{2,1,0:T(8,128)(2,1)S(1)}, bf16[4,96,128]{2,1,0:T(8,128)(2,1)S(1)}, u32[]{:S(2)}, u32[]{:S(2)}) %collective-permute-start.18) | collective-permute-done | bytes 98336 | tf_op jit(solution)/shard_map/ppermute | solution.py:23
  49.1 1.6 %collective-permute-start.21 = (f32[8,128]{1,0:T(8,128)S(1)}, f32[8,128]{1,0:T(8,128)S(1)}, u32[]{:S(2)}, u32[]{:S(2)}) collective-permute-start(f32[8,128]{1,0:T(8,128)S(1)} %get-tuple-element.44.refs_0_), channel_id=1, source_target_pairs={{0,12},{1,13},{2,14},{3,15},{4,8},{5,9},{6,10},{7,11},{8,4},{9,5},... | collective-permute-start | bytes 12296 | tf_op jit(solution)/shard_map/ppermute | solution.py:23
  50.7 2.8 %collective-permute-start.19 = (f32[8,128]{1,0:T(8,128)S(1)}, f32[8,128]{1,0:T(8,128)S(1)}, u32[]{:S(2)}, u32[]{:S(2)}) collective-permute-start(f32[8,128]{1,0:T(8,128)S(1)} %get-tuple-element.44.refs_0_), channel_id=1, source_target_pairs={{0,4},{1,5},{2,6},{3,7},{4,0},{5,1},{6,2},{7,3},{8,12},{9,13},{10,... | collective-permute-start | bytes 12296 | tf_op jit(solution)/shard_map/ppermute | solution.py:23
  59.2 2.0 %collective-permute-start.27 = (bf16[8,96,128]{2,1,0:T(8,128)(2,1)S(1)}, bf16[8,96,128]{2,1,0:T(8,128)(2,1)S(1)}, u32[]{:S(2)}, u32[]{:S(2)}) collective-permute-start(bf16[8,96,128]{2,1,0:T(8,128)(2,1)S(1)} %get-tuple-element.46.own_ref), channel_id=1, source_target_pairs={{8,0},{9,1},{10,2},{11,3},{12,4},{13,5},{14,6},{15,7},{0,8},{1,9},... | collective-permute-start | bytes 589832 | tf_op jit(solution)/shard_map/ppermute | solution.py:23
  62.8 8.4 %collective-permute-done.27.refs_6_ = bf16[8,96,128]{2,1,0:T(8,128)(2,1)S(1)} collective-permute-done((bf16[8,96,128]{2,1,0:T(8,128)(2,1)S(1)}, bf16[8,96,128]{2,1,0:T(8,128)(2,1)S(1)}, u32[]{:S(2)}, u32[]{:S(2)}) %collective-permute-start.27) | collective-permute-done | bytes 196640 | tf_op jit(solution)/shard_map/ppermute | solution.py:23
  71.9 1.9 %collective-permute-start.30 = (f32[8,128]{1,0:T(8,128)S(1)}, f32[8,128]{1,0:T(8,128)S(1)}, u32[]{:S(2)}, u32[]{:S(2)}) collective-permute-start(f32[8,128]{1,0:T(8,128)S(1)} %get-tuple-element.49.refs_0_), channel_id=1, source_target_pairs={{0,12},{1,13},{2,14},{3,15},{4,8},{5,9},{6,10},{7,11},{8,4},{9,5},... | collective-permute-start | bytes 12296 | tf_op jit(solution)/shard_map/ppermute | solution.py:23
  73.8 2.5 %collective-permute-start.28 = (f32[8,128]{1,0:T(8,128)S(1)}, f32[8,128]{1,0:T(8,128)S(1)}, u32[]{:S(2)}, u32[]{:S(2)}) collective-permute-start(f32[8,128]{1,0:T(8,128)S(1)} %get-tuple-element.49.refs_0_), channel_id=1, source_target_pairs={{0,4},{1,5},{2,6},{3,7},{4,0},{5,1},{6,2},{7,3},{8,12},{9,13},{10,... | collective-permute-start | bytes 12296 | tf_op jit(solution)/shard_map/ppermute | solution.py:23
  78.4 1.3 %collective-permute-start.32 = (f32[8,128]{1,0:T(8,128)S(1)}, f32[8,128]{1,0:T(8,128)S(1)}, u32[]{:S(2)}, u32[]{:S(2)}) collective-permute-start(f32[8,128]{1,0:T(8,128)S(1)} %shard_map.76.refs_0_), channel_id=1, source_target_pairs={{0,2},{1,3},{2,0},{3,1},{4,6},{5,7},{6,4},{7,5},{8,10},{9,11},{10,... | collective-permute-start | bytes 12296 | tf_op jit(solution)/shard_map/ppermute | solution.py:23
  82.3 2.0 %collective-permute-start.36 = (bf16[8,96,128]{2,1,0:T(8,128)(2,1)S(1)}, bf16[8,96,128]{2,1,0:T(8,128)(2,1)S(1)}, u32[]{:S(2)}, u32[]{:S(2)}) collective-permute-start(bf16[8,96,128]{2,1,0:T(8,128)(2,1)S(1)} %get-tuple-element.54.own_ref), channel_id=1, source_target_pairs={{8,0},{9,1},{10,2},{11,3},{12,4},{13,5},{14,6},{15,7},{0,8},{1,9},... | collective-permute-start | bytes 589832 | tf_op jit(solution)/shard_map/ppermute | solution.py:23
  86.2 8.3 %collective-permute-done.36.refs_6_ = bf16[8,96,128]{2,1,0:T(8,128)(2,1)S(1)} collective-permute-done((bf16[8,96,128]{2,1,0:T(8,128)(2,1)S(1)}, bf16[8,96,128]{2,1,0:T(8,128)(2,1)S(1)}, u32[]{:S(2)}, u32[]{:S(2)}) %collective-permute-start.36) | collective-permute-done | bytes 196640 | tf_op jit(solution)/shard_map/ppermute | solution.py:23
  95.1 2.0 %collective-permute-start.39 = (f32[8,128]{1,0:T(8,128)S(1)}, f32[8,128]{1,0:T(8,128)S(1)}, u32[]{:S(2)}, u32[]{:S(2)}) collective-permute-start(f32[8,128]{1,0:T(8,128)S(1)} %get-tuple-element.57.refs_0_), channel_id=1, source_target_pairs={{0,12},{1,13},{2,14},{3,15},{4,8},{5,9},{6,10},{7,11},{8,4},{9,5},... | collective-permute-start | bytes 12296 | tf_op jit(solution)/shard_map/ppermute | solution.py:23
  97.1 2.4 %collective-permute-start.37 = (f32[8,128]{1,0:T(8,128)S(1)}, f32[8,128]{1,0:T(8,128)S(1)}, u32[]{:S(2)}, u32[]{:S(2)}) collective-permute-start(f32[8,128]{1,0:T(8,128)S(1)} %get-tuple-element.57.refs_0_), channel_id=1, source_target_pairs={{0,4},{1,5},{2,6},{3,7},{4,0},{5,1},{6,2},{7,3},{8,12},{9,13},{10,... | collective-permute-start | bytes 12296 | tf_op jit(solution)/shard_map/ppermute | solution.py:23
  (92 shorter events, 36.5 us)
Async XLA Ops:
  2.3 12.6 %collective-permute-start.1 = (bf16[8,8,96,128]{3,2,1,0:T(8,128)(2,1)S(1)}, bf16[8,8,96,128]{3,2,1,0:T(8,128)(2,1)S(1)}, u32[]{:S(2)}, u32[]{:S(2)}) collective-permute-start(bf16[8,8,96,128]{3,2,1,0:T(8,128)(2,1)S(1)} %dynamic-slice_bitcast_fusion), channel_id=1, source_target_pairs={{0,1},{1,0},{2,3},{3,2},{4,5},{5,4},{6,7},{7,6},{8,9},{9,8},{10,11... | collective-permute-start | bytes 4718600 | tf_op jit(solution)/shard_map/ppermute | solution.py:23
  3.0 7.9 %collective-permute-start = (bf16[16,2304]{1,0:T(8,128)(2,1)S(1)}, bf16[16,2304]{1,0:T(8,128)(2,1)S(1)}, u32[]{:S(2)}, u32[]{:S(2)}) collective-permute-start(bf16[16,2304]{1,0:T(8,128)(2,1)S(1)} %get-tuple-element.33), channel_id=1, source_target_pairs={{0,12},{1,13},{2,14},{3,15},{4,8},{5,9},{6,10},{7,11},{8,4},{9,5},... | collective-permute-start | bytes 221192 | tf_op jit(solution)/shard_map/ppermute | solution.py:23
  7.6 7.1 %collective-permute-start.3 = (bf16[16,2304]{1,0:T(8,128)(2,1)S(1)}, bf16[16,2304]{1,0:T(8,128)(2,1)S(1)}, u32[]{:S(2)}, u32[]{:S(2)}) collective-permute-start(bf16[16,2304]{1,0:T(8,128)(2,1)S(1)} %get-tuple-element.34), channel_id=1, source_target_pairs={{0,6},{1,7},{2,4},{3,5},{4,2},{5,3},{6,0},{7,1},{8,14},{9,15},{10,... | collective-permute-start | bytes 221192 | tf_op jit(solution)/shard_map/ppermute | solution.py:23
  8.1 9.7 %collective-permute-start.5 = (bf16[16,2304]{1,0:T(8,128)(2,1)S(1)}, bf16[16,2304]{1,0:T(8,128)(2,1)S(1)}, u32[]{:S(2)}, u32[]{:S(2)}) collective-permute-start(bf16[16,2304]{1,0:T(8,128)(2,1)S(1)} %get-tuple-element.35), channel_id=1, source_target_pairs={{0,14},{1,15},{2,12},{3,13},{4,10},{5,11},{6,8},{7,9},{8,6},{9,7},... | collective-permute-start | bytes 221192 | tf_op jit(solution)/shard_map/ppermute | solution.py:23
  9.4 10.6 %collective-permute-start.13 = (bf16[16,2304]{1,0:T(8,128)(2,1)S(1)}, bf16[16,2304]{1,0:T(8,128)(2,1)S(1)}, u32[]{:S(2)}, u32[]{:S(2)}) collective-permute-start(bf16[16,2304]{1,0:T(8,128)(2,1)S(1)} %get-tuple-element.39), channel_id=1, source_target_pairs={{0,4},{1,5},{2,6},{3,7},{4,0},{5,1},{6,2},{7,3},{8,12},{9,13},{10,... | collective-permute-start | bytes 221192 | tf_op jit(solution)/shard_map/ppermute | solution.py:23
  10.8 11.3 %collective-permute-start.7 = (bf16[16,2304]{1,0:T(8,128)(2,1)S(1)}, bf16[16,2304]{1,0:T(8,128)(2,1)S(1)}, u32[]{:S(2)}, u32[]{:S(2)}) collective-permute-start(bf16[16,2304]{1,0:T(8,128)(2,1)S(1)} %get-tuple-element.36), channel_id=1, source_target_pairs={{0,10},{1,11},{2,8},{3,9},{4,14},{5,15},{6,12},{7,13},{8,2},{9,3},... | collective-permute-start | bytes 221192 | tf_op jit(solution)/shard_map/ppermute | solution.py:23
  14.8 10.9 %collective-permute-start.9 = (bf16[16,2304]{1,0:T(8,128)(2,1)S(1)}, bf16[16,2304]{1,0:T(8,128)(2,1)S(1)}, u32[]{:S(2)}, u32[]{:S(2)}) collective-permute-start(bf16[16,2304]{1,0:T(8,128)(2,1)S(1)} %get-tuple-element.37), channel_id=1, source_target_pairs={{0,8},{1,9},{2,10},{3,11},{4,12},{5,13},{6,14},{7,15},{8,0},{9,1},... | collective-permute-start | bytes 221192 | tf_op jit(solution)/shard_map/ppermute | solution.py:23
  14.9 12.4 %collective-permute-start.11 = (bf16[16,2304]{1,0:T(8,128)(2,1)S(1)}, bf16[16,2304]{1,0:T(8,128)(2,1)S(1)}, u32[]{:S(2)}, u32[]{:S(2)}) collective-permute-start(bf16[16,2304]{1,0:T(8,128)(2,1)S(1)} %get-tuple-element.38), channel_id=1, source_target_pairs={{0,2},{1,3},{2,0},{3,1},{4,6},{5,7},{6,4},{7,5},{8,10},{9,11},{10,... | collective-permute-start | bytes 221192 | tf_op jit(solution)/shard_map/ppermute | solution.py:23
  17.9 12.4 %collective-permute-start.2 = (f32[96,128]{1,0:T(8,128)S(1)}, f32[96,128]{1,0:T(8,128)S(1)}, u32[]{:S(2)}, u32[]{:S(2)}) collective-permute-start(f32[96,128]{1,0:T(8,128)S(1)} %shard_map.60), channel_id=1, source_target_pairs={{0,12},{1,13},{2,14},{3,15},{4,8},{5,9},{6,10},{7,11},{8,4},{9,5},... | collective-permute-start | bytes 147464 | tf_op jit(solution)/shard_map/ppermute | solution.py:23
  20.0 11.2 %collective-permute-start.4 = (f32[96,128]{1,0:T(8,128)S(1)}, f32[96,128]{1,0:T(8,128)S(1)}, u32[]{:S(2)}, u32[]{:S(2)}) collective-permute-start(f32[96,128]{1,0:T(8,128)S(1)} %shard_map.61), channel_id=1, source_target_pairs={{0,6},{1,7},{2,4},{3,5},{4,2},{5,3},{6,0},{7,1},{8,14},{9,15},{10,... | collective-permute-start | bytes 147464 | tf_op jit(solution)/shard_map/ppermute | solution.py:23
  22.1 9.6 %collective-permute-start.6 = (f32[96,128]{1,0:T(8,128)S(1)}, f32[96,128]{1,0:T(8,128)S(1)}, u32[]{:S(2)}, u32[]{:S(2)}) collective-permute-start(f32[96,128]{1,0:T(8,128)S(1)} %shard_map.62), channel_id=1, source_target_pairs={{0,14},{1,15},{2,12},{3,13},{4,10},{5,11},{6,8},{7,9},{8,6},{9,7},... | collective-permute-start | bytes 147464 | tf_op jit(solution)/shard_map/ppermute | solution.py:23
  25.7 6.1 %collective-permute-start.8 = (f32[96,128]{1,0:T(8,128)S(1)}, f32[96,128]{1,0:T(8,128)S(1)}, u32[]{:S(2)}, u32[]{:S(2)}) collective-permute-start(f32[96,128]{1,0:T(8,128)S(1)} %shard_map.63), channel_id=1, source_target_pairs={{0,10},{1,11},{2,8},{3,9},{4,14},{5,15},{6,12},{7,13},{8,2},{9,3},... | collective-permute-start | bytes 147464 | tf_op jit(solution)/shard_map/ppermute | solution.py:23
  35.4 13.1 %collective-permute-start.16 = (bf16[8,96,128]{2,1,0:T(8,128)(2,1)S(1)}, bf16[8,96,128]{2,1,0:T(8,128)(2,1)S(1)}, u32[]{:S(2)}, u32[]{:S(2)}) collective-permute-start(bf16[8,96,128]{2,1,0:T(8,128)(2,1)S(1)} %get-tuple-element.41.own_ref), channel_id=1, source_target_pairs={{0,7},{1,2},{2,1},{3,4},{4,3},{5,6},{6,5},{7,0},{8,15},{9,10},{10,... | collective-permute-start | bytes 589832 | tf_op jit(solution)/shard_map/ppermute | solution.py:23
  35.4 13.0 %collective-permute-start.15 = (bf16[8,96,128]{2,1,0:T(8,128)(2,1)S(1)}, bf16[8,96,128]{2,1,0:T(8,128)(2,1)S(1)}, u32[]{:S(2)}, u32[]{:S(2)}) collective-permute-start(bf16[8,96,128]{2,1,0:T(8,128)(2,1)S(1)} %get-tuple-element.41.own_ref), channel_id=1, source_target_pairs={{0,1},{1,0},{2,3},{3,2},{4,5},{5,4},{6,7},{7,6},{8,9},{9,8},{10,11... | collective-permute-start | bytes 589832 | tf_op jit(solution)/shard_map/ppermute | solution.py:23
  36.7 10.1 %collective-permute-start.17 = (bf16[4,96,128]{2,1,0:T(8,128)(2,1)S(1)}, bf16[4,96,128]{2,1,0:T(8,128)(2,1)S(1)}, u32[]{:S(2)}, u32[]{:S(2)}) collective-permute-start(bf16[4,96,128]{2,1,0:T(8,128)(2,1)S(1)} %shard_map.70), channel_id=1, source_target_pairs={{8,0},{9,1},{10,2},{11,3},{12,4},{13,5},{14,6},{15,7},{0,8},{1,9},... | collective-permute-start | bytes 294920 | tf_op jit(solution)/shard_map/ppermute | solution.py:23
  37.4 11.1 %collective-permute-start.18 = (bf16[4,96,128]{2,1,0:T(8,128)(2,1)S(1)}, bf16[4,96,128]{2,1,0:T(8,128)(2,1)S(1)}, u32[]{:S(2)}, u32[]{:S(2)}) collective-permute-start(bf16[4,96,128]{2,1,0:T(8,128)(2,1)S(1)} %get-tuple-element.43), channel_id=1, source_target_pairs={{8,0},{9,1},{10,2},{11,3},{12,4},{13,5},{14,6},{15,7},{0,8},{1,9},... | collective-permute-start | bytes 294920 | tf_op jit(solution)/shard_map/ppermute | solution.py:23
  49.1 5.5 %collective-permute-start.21 = (f32[8,128]{1,0:T(8,128)S(1)}, f32[8,128]{1,0:T(8,128)S(1)}, u32[]{:S(2)}, u32[]{:S(2)}) collective-permute-start(f32[8,128]{1,0:T(8,128)S(1)} %get-tuple-element.44.refs_0_), channel_id=1, source_target_pairs={{0,12},{1,13},{2,14},{3,15},{4,8},{5,9},{6,10},{7,11},{8,4},{9,5},... | collective-permute-start | bytes 12296 | tf_op jit(solution)/shard_map/ppermute | solution.py:23
  59.2 12.1 %collective-permute-start.27 = (bf16[8,96,128]{2,1,0:T(8,128)(2,1)S(1)}, bf16[8,96,128]{2,1,0:T(8,128)(2,1)S(1)}, u32[]{:S(2)}, u32[]{:S(2)}) collective-permute-start(bf16[8,96,128]{2,1,0:T(8,128)(2,1)S(1)} %get-tuple-element.46.own_ref), channel_id=1, source_target_pairs={{8,0},{9,1},{10,2},{11,3},{12,4},{13,5},{14,6},{15,7},{0,8},{1,9},... | collective-permute-start | bytes 589832 | tf_op jit(solution)/shard_map/ppermute | solution.py:23
  61.2 10.1 %collective-permute-start.26 = (bf16[8,96,128]{2,1,0:T(8,128)(2,1)S(1)}, bf16[8,96,128]{2,1,0:T(8,128)(2,1)S(1)}, u32[]{:S(2)}, u32[]{:S(2)}) collective-permute-start(bf16[8,96,128]{2,1,0:T(8,128)(2,1)S(1)} %get-tuple-element.46.own_ref), channel_id=1, source_target_pairs={{0,7},{1,2},{2,1},{3,4},{4,3},{5,6},{6,5},{7,0},{8,15},{9,10},{10,... | collective-permute-start | bytes 589832 | tf_op jit(solution)/shard_map/ppermute | solution.py:23
  61.7 9.5 %collective-permute-start.25 = (bf16[8,96,128]{2,1,0:T(8,128)(2,1)S(1)}, bf16[8,96,128]{2,1,0:T(8,128)(2,1)S(1)}, u32[]{:S(2)}, u32[]{:S(2)}) collective-permute-start(bf16[8,96,128]{2,1,0:T(8,128)(2,1)S(1)} %get-tuple-element.46.own_ref), channel_id=1, source_target_pairs={{0,1},{1,0},{2,3},{3,2},{4,5},{5,4},{6,7},{7,6},{8,9},{9,8},{10,11... | collective-permute-start | bytes 589832 | tf_op jit(solution)/shard_map/ppermute | solution.py:23
  82.3 12.1 %collective-permute-start.36 = (bf16[8,96,128]{2,1,0:T(8,128)(2,1)S(1)}, bf16[8,96,128]{2,1,0:T(8,128)(2,1)S(1)}, u32[]{:S(2)}, u32[]{:S(2)}) collective-permute-start(bf16[8,96,128]{2,1,0:T(8,128)(2,1)S(1)} %get-tuple-element.54.own_ref), channel_id=1, source_target_pairs={{8,0},{9,1},{10,2},{11,3},{12,4},{13,5},{14,6},{15,7},{0,8},{1,9},... | collective-permute-start | bytes 589832 | tf_op jit(solution)/shard_map/ppermute | solution.py:23
  84.3 10.1 %collective-permute-start.35 = (bf16[8,96,128]{2,1,0:T(8,128)(2,1)S(1)}, bf16[8,96,128]{2,1,0:T(8,128)(2,1)S(1)}, u32[]{:S(2)}, u32[]{:S(2)}) collective-permute-start(bf16[8,96,128]{2,1,0:T(8,128)(2,1)S(1)} %get-tuple-element.54.own_ref), channel_id=1, source_target_pairs={{0,7},{1,2},{2,1},{3,4},{4,3},{5,6},{6,5},{7,0},{8,15},{9,10},{10,... | collective-permute-start | bytes 589832 | tf_op jit(solution)/shard_map/ppermute | solution.py:23
  84.9 9.6 %collective-permute-start.34 = (bf16[8,96,128]{2,1,0:T(8,128)(2,1)S(1)}, bf16[8,96,128]{2,1,0:T(8,128)(2,1)S(1)}, u32[]{:S(2)}, u32[]{:S(2)}) collective-permute-start(bf16[8,96,128]{2,1,0:T(8,128)(2,1)S(1)} %get-tuple-element.54.own_ref), channel_id=1, source_target_pairs={{0,1},{1,0},{2,3},{3,2},{4,5},{5,4},{6,7},{7,6},{8,9},{9,8},{10,11... | collective-permute-start | bytes 589832 | tf_op jit(solution)/shard_map/ppermute | solution.py:23
  95.1 5.5 %collective-permute-start.39 = (f32[8,128]{1,0:T(8,128)S(1)}, f32[8,128]{1,0:T(8,128)S(1)}, u32[]{:S(2)}, u32[]{:S(2)}) collective-permute-start(f32[8,128]{1,0:T(8,128)S(1)} %get-tuple-element.57.refs_0_), channel_id=1, source_target_pairs={{0,12},{1,13},{2,14},{3,15},{4,8},{5,9},{6,10},{7,11},{8,4},{9,5},... | collective-permute-start | bytes 12296 | tf_op jit(solution)/shard_map/ppermute | solution.py:23
  (22 other events, 101.3 us)

commit v3 on v2

--- a/solution.py
+++ b/solution.py
@@ -23,12 +23,12 @@
     return lax.ppermute(value, "ta", pairs)
 
 
-def whole_call(body, out_shape, operands, specs, scratch=()):
+def whole_call(body, out_shape, operands, specs, scratch=(), out=VMEM):
     return pl.pallas_call(
         body,
         out_shape=out_shape,
         in_specs=specs,
-        out_specs=jax.tree.map(lambda _: VMEM, out_shape),
+        out_specs=jax.tree.map(lambda _: out, out_shape),
         scratch_shapes=list(scratch),
         compiler_params=pltpu.CompilerParams(vmem_limit_bytes=6 * 1024 * 1024),
     )(*operands)
@@ -321,8 +321,9 @@
     basis_q = [refs.pop(0) for _ in range(count)]
     basis_p = [refs.pop(0) for _ in range(count)]
     solution_ref, known_ref = (refs.pop(0), refs.pop(0)) if count else (None, None)
+    copies = []
     if last:
-        new_solution, new_residual = refs
+        whole_solution, whole_residual, new_solution, new_residual, semaphores = refs
     else:
         new_solution, new_residual, rounded_ref, unit_q_ref, unit_p_ref, new_known = refs
     site_count = mapped_ref.shape[0]
@@ -386,10 +387,21 @@
         new_solution[site] = change if solution_ref is None else solution_ref[site] + change
         held = held - scaled(unit_q, *alpha, half)
         new_residual[site] = held
-        if not last:
+        if last:
+            pairs = ((new_solution, whole_solution), (new_residual, whole_residual))
+            for number, (local, whole) in enumerate(pairs):
+                copies.append(
+                    pltpu.make_async_copy(
+                        local.at[site], whole.at[site], semaphores.at[number, site]
+                    )
+                )
+                copies[-1].start()
+        else:
             rounded_ref[site] = held.astype(jnp.bfloat16)
             unit_q_ref[site] = unit_q
             unit_p_ref[site] = unit_p
+    for copy in copies:
+        copy.wait()
 
 
 def add_pairs(refs):
@@ -499,6 +511,14 @@
             results,
             operands,
             [VMEM] * len(operands),
+            [
+                pltpu.VMEM(full.shape, jnp.float32),
+                pltpu.VMEM(full.shape, jnp.float32),
+                pltpu.SemaphoreType.DMA((2, site_count)),
+            ]
+            if last
+            else [],
+            out=pl.BlockSpec(memory_space=pl.ANY) if last else VMEM,
         )
         total, residual = outs[:2]
         if not last:

time: 107 us -> 107 us (level)
  no operation moved by 1% of the time
where the time goes in v3:
time: 107 us
  starting transfers between devices  53.6 us (50%)
  waiting for transfers between devices  40.9 us (38%)
  Pallas kernels  8.73 us (8%)
  local copies, waits for them, and re-layouts  1.69 us (2%)
  between operations  1.58 us (1%)
    ppermute x43, starting transfers between devices, send(): return lax.ppermute(value, 'ta', pairs)  53.6 us
    ppermute x43, waiting for transfers between devices, send(): return lax.ppermute(value, 'ta', pairs)  40.9 us
    pallas_call x23, Pallas kernels, whole_call(): pl.pallas_call(body, out_shape=out_shape, in_specs=specs, out_specs=jax.t...  8.73 us
  transfers between devices with their start and end apart: 43, of which 22 were waited for; matrix products, arithmetic and copies ran while one was open for 0% of the time, Pallas kernels for 5%

profile of v3, /device:TPU:0, one launch (start us, length us, event | category | flops | bytes accessed | tf_op | source)
XLA Modules:
  0.0 106.5 jit_solution(9235064771361435943)
XLA Ops:
  0.7 1.7 %dynamic-slice_bitcast_fusion = bf16[8,8,96,128]{3,2,1,0:T(8,128)(2,1)S(1)} fusion(bf16[8,2,8,96,128]{4,3,2,1,0:T(8,128)(2,1)} %bitcast.11, s32[]{:T(128)S(6)} %select_n.12), kind=kLoop, calls=%fused_computation | loop fusion | bytes 3145732 | tf_op jit(solution)/shard_map/jit(dynamic_index_in_dim)/squeeze | solution.py:146
  3.0 4.7 %collective-permute-start = (bf16[16,2304]{1,0:T(8,128)(2,1)S(1)}, bf16[16,2304]{1,0:T(8,128)(2,1)S(1)}, u32[]{:S(2)}, u32[]{:S(2)}) collective-permute-start(bf16[16,2304]{1,0:T(8,128)(2,1)S(1)} %get-tuple-element.33), channel_id=1, source_target_pairs={{0,12},{1,13},{2,14},{3,15},{4,8},{5,9},{6,10},{7,11},{8,4},{9,5},... | collective-permute-start | bytes 221192 | tf_op jit(solution)/shard_map/ppermute | solution.py:23
  8.1 1.3 %collective-permute-start.5 = (bf16[16,2304]{1,0:T(8,128)(2,1)S(1)}, bf16[16,2304]{1,0:T(8,128)(2,1)S(1)}, u32[]{:S(2)}, u32[]{:S(2)}) collective-permute-start(bf16[16,2304]{1,0:T(8,128)(2,1)S(1)} %get-tuple-element.35), channel_id=1, source_target_pairs={{0,14},{1,15},{2,12},{3,13},{4,10},{5,11},{6,8},{7,9},{8,6},{9,7},... | collective-permute-start | bytes 221192 | tf_op jit(solution)/shard_map/ppermute | solution.py:23
  10.8 2.6 %collective-permute-start.7 = (bf16[16,2304]{1,0:T(8,128)(2,1)S(1)}, bf16[16,2304]{1,0:T(8,128)(2,1)S(1)}, u32[]{:S(2)}, u32[]{:S(2)}) collective-permute-start(bf16[16,2304]{1,0:T(8,128)(2,1)S(1)} %get-tuple-element.36), channel_id=1, source_target_pairs={{0,10},{1,11},{2,8},{3,9},{4,14},{5,15},{6,12},{7,13},{8,2},{9,3},... | collective-permute-start | bytes 221192 | tf_op jit(solution)/shard_map/ppermute | solution.py:23
  13.4 1.3 %collective-permute-done.3.refs_1_ = bf16[16,2304]{1,0:T(8,128)(2,1)S(1)} collective-permute-done((bf16[16,2304]{1,0:T(8,128)(2,1)S(1)}, bf16[16,2304]{1,0:T(8,128)(2,1)S(1)}, u32[]{:S(2)}, u32[]{:S(2)}) %collective-permute-start.3) | collective-permute-done | bytes 73760 | tf_op jit(solution)/shard_map/ppermute | solution.py:23
  14.9 2.0 %collective-permute-start.11 = (bf16[16,2304]{1,0:T(8,128)(2,1)S(1)}, bf16[16,2304]{1,0:T(8,128)(2,1)S(1)}, u32[]{:S(2)}, u32[]{:S(2)}) collective-permute-start(bf16[16,2304]{1,0:T(8,128)(2,1)S(1)} %get-tuple-element.38), channel_id=1, source_target_pairs={{0,2},{1,3},{2,0},{3,1},{4,6},{5,7},{6,4},{7,5},{8,10},{9,11},{10,... | collective-permute-start | bytes 221192 | tf_op jit(solution)/shard_map/ppermute | solution.py:23
  17.9 2.1 %collective-permute-start.2 = (f32[96,128]{1,0:T(8,128)S(1)}, f32[96,128]{1,0:T(8,128)S(1)}, u32[]{:S(2)}, u32[]{:S(2)}) collective-permute-start(f32[96,128]{1,0:T(8,128)S(1)} %shard_map.60), channel_id=1, source_target_pairs={{0,12},{1,13},{2,14},{3,15},{4,8},{5,9},{6,10},{7,11},{8,4},{9,5},... | collective-permute-start | bytes 147464 | tf_op jit(solution)/shard_map/ppermute | solution.py:23
  22.1 3.1 %collective-permute-start.6 = (f32[96,128]{1,0:T(8,128)S(1)}, f32[96,128]{1,0:T(8,128)S(1)}, u32[]{:S(2)}, u32[]{:S(2)}) collective-permute-start(f32[96,128]{1,0:T(8,128)S(1)} %shard_map.62), channel_id=1, source_target_pairs={{0,14},{1,15},{2,12},{3,13},{4,10},{5,11},{6,8},{7,9},{8,6},{9,7},... | collective-permute-start | bytes 147464 | tf_op jit(solution)/shard_map/ppermute | solution.py:23
  27.4 2.4 %collective-permute-start.10 = (f32[96,128]{1,0:T(8,128)S(1)}, f32[96,128]{1,0:T(8,128)S(1)}, u32[]{:S(2)}, u32[]{:S(2)}) collective-permute-start(f32[96,128]{1,0:T(8,128)S(1)} %shard_map.64), channel_id=1, source_target_pairs={{0,8},{1,9},{2,10},{3,11},{4,12},{5,13},{6,14},{7,15},{8,0},{9,1},... | collective-permute-start | bytes 147464 | tf_op jit(solution)/shard_map/ppermute | solution.py:23
  32.4 2.0 %collective-permute-done.12.refs_6_ = f32[96,128]{1,0:T(8,128)S(1)} collective-permute-done((f32[96,128]{1,0:T(8,128)S(1)}, f32[96,128]{1,0:T(8,128)S(1)}, u32[]{:S(2)}, u32[]{:S(2)}) %collective-permute-start.12) | collective-permute-done | bytes 49184 | tf_op jit(solution)/shard_map/ppermute | solution.py:23
  37.4 2.4 %collective-permute-start.18 = (bf16[4,96,128]{2,1,0:T(8,128)(2,1)S(1)}, bf16[4,96,128]{2,1,0:T(8,128)(2,1)S(1)}, u32[]{:S(2)}, u32[]{:S(2)}) collective-permute-start(bf16[4,96,128]{2,1,0:T(8,128)(2,1)S(1)} %get-tuple-element.43), channel_id=1, source_target_pairs={{8,0},{9,1},{10,2},{11,3},{12,4},{13,5},{14,6},{15,7},{0,8},{1,9},... | collective-permute-start | bytes 294920 | tf_op jit(solution)/shard_map/ppermute | solution.py:23
  40.9 5.9 %collective-permute-done.17.refs_6_ = bf16[4,96,128]{2,1,0:T(8,128)(2,1)S(1)} collective-permute-done((bf16[4,96,128]{2,1,0:T(8,128)(2,1)S(1)}, bf16[4,96,128]{2,1,0:T(8,128)(2,1)S(1)}, u32[]{:S(2)}, u32[]{:S(2)}) %collective-permute-start.17) | collective-permute-done | bytes 98336 | tf_op jit(solution)/shard_map/ppermute | solution.py:23
  46.8 1.6 %collective-permute-done.18.refs_7_ = bf16[4,96,128]{2,1,0:T(8,128)(2,1)S(1)} collective-permute-done((bf16[4,96,128]{2,1,0:T(8,128)(2,1)S(1)}, bf16[4,96,128]{2,1,0:T(8,128)(2,1)S(1)}, u32[]{:S(2)}, u32[]{:S(2)}) %collective-permute-start.18) | collective-permute-done | bytes 98336 | tf_op jit(solution)/shard_map/ppermute | solution.py:23
  49.1 1.6 %collective-permute-start.21 = (f32[8,128]{1,0:T(8,128)S(1)}, f32[8,128]{1,0:T(8,128)S(1)}, u32[]{:S(2)}, u32[]{:S(2)}) collective-permute-start(f32[8,128]{1,0:T(8,128)S(1)} %get-tuple-element.44.refs_0_), channel_id=1, source_target_pairs={{0,12},{1,13},{2,14},{3,15},{4,8},{5,9},{6,10},{7,11},{8,4},{9,5},... | collective-permute-start | bytes 12296 | tf_op jit(solution)/shard_map/ppermute | solution.py:23
  50.7 2.8 %collective-permute-start.19 = (f32[8,128]{1,0:T(8,128)S(1)}, f32[8,128]{1,0:T(8,128)S(1)}, u32[]{:S(2)}, u32[]{:S(2)}) collective-permute-start(f32[8,128]{1,0:T(8,128)S(1)} %get-tuple-element.44.refs_0_), channel_id=1, source_target_pairs={{0,4},{1,5},{2,6},{3,7},{4,0},{5,1},{6,2},{7,3},{8,12},{9,13},{10,... | collective-permute-start | bytes 12296 | tf_op jit(solution)/shard_map/ppermute | solution.py:23
  59.2 2.0 %collective-permute-start.27 = (bf16[8,96,128]{2,1,0:T(8,128)(2,1)S(1)}, bf16[8,96,128]{2,1,0:T(8,128)(2,1)S(1)}, u32[]{:S(2)}, u32[]{:S(2)}) collective-permute-start(bf16[8,96,128]{2,1,0:T(8,128)(2,1)S(1)} %get-tuple-element.46.own_ref), channel_id=1, source_target_pairs={{8,0},{9,1},{10,2},{11,3},{12,4},{13,5},{14,6},{15,7},{0,8},{1,9},... | collective-permute-start | bytes 589832 | tf_op jit(solution)/shard_map/ppermute | solution.py:23
  62.8 8.4 %collective-permute-done.27.refs_6_ = bf16[8,96,128]{2,1,0:T(8,128)(2,1)S(1)} collective-permute-done((bf16[8,96,128]{2,1,0:T(8,128)(2,1)S(1)}, bf16[8,96,128]{2,1,0:T(8,128)(2,1)S(1)}, u32[]{:S(2)}, u32[]{:S(2)}) %collective-permute-start.27) | collective-permute-done | bytes 196640 | tf_op jit(solution)/shard_map/ppermute | solution.py:23
  71.9 1.9 %collective-permute-start.30 = (f32[8,128]{1,0:T(8,128)S(1)}, f32[8,128]{1,0:T(8,128)S(1)}, u32[]{:S(2)}, u32[]{:S(2)}) collective-permute-start(f32[8,128]{1,0:T(8,128)S(1)} %get-tuple-element.49.refs_0_), channel_id=1, source_target_pairs={{0,12},{1,13},{2,14},{3,15},{4,8},{5,9},{6,10},{7,11},{8,4},{9,5},... | collective-permute-start | bytes 12296 | tf_op jit(solution)/shard_map/ppermute | solution.py:23
  73.8 2.5 %collective-permute-start.28 = (f32[8,128]{1,0:T(8,128)S(1)}, f32[8,128]{1,0:T(8,128)S(1)}, u32[]{:S(2)}, u32[]{:S(2)}) collective-permute-start(f32[8,128]{1,0:T(8,128)S(1)} %get-tuple-element.49.refs_0_), channel_id=1, source_target_pairs={{0,4},{1,5},{2,6},{3,7},{4,0},{5,1},{6,2},{7,3},{8,12},{9,13},{10,... | collective-permute-start | bytes 12296 | tf_op jit(solution)/shard_map/ppermute | solution.py:23
  78.4 1.3 %collective-permute-start.32 = (f32[8,128]{1,0:T(8,128)S(1)}, f32[8,128]{1,0:T(8,128)S(1)}, u32[]{:S(2)}, u32[]{:S(2)}) collective-permute-start(f32[8,128]{1,0:T(8,128)S(1)} %shard_map.76.refs_0_), channel_id=1, source_target_pairs={{0,2},{1,3},{2,0},{3,1},{4,6},{5,7},{6,4},{7,5},{8,10},{9,11},{10,... | collective-permute-start | bytes 12296 | tf_op jit(solution)/shard_map/ppermute | solution.py:23
  82.3 2.0 %collective-permute-start.36 = (bf16[8,96,128]{2,1,0:T(8,128)(2,1)S(1)}, bf16[8,96,128]{2,1,0:T(8,128)(2,1)S(1)}, u32[]{:S(2)}, u32[]{:S(2)}) collective-permute-start(bf16[8,96,128]{2,1,0:T(8,128)(2,1)S(1)} %get-tuple-element.54.own_ref), channel_id=1, source_target_pairs={{8,0},{9,1},{10,2},{11,3},{12,4},{13,5},{14,6},{15,7},{0,8},{1,9},... | collective-permute-start | bytes 589832 | tf_op jit(solution)/shard_map/ppermute | solution.py:23
  86.2 8.3 %collective-permute-done.36.refs_6_ = bf16[8,96,128]{2,1,0:T(8,128)(2,1)S(1)} collective-permute-done((bf16[8,96,128]{2,1,0:T(8,128)(2,1)S(1)}, bf16[8,96,128]{2,1,0:T(8,128)(2,1)S(1)}, u32[]{:S(2)}, u32[]{:S(2)}) %collective-permute-start.36) | collective-permute-done | bytes 196640 | tf_op jit(solution)/shard_map/ppermute | solution.py:23
  95.1 2.0 %collective-permute-start.39 = (f32[8,128]{1,0:T(8,128)S(1)}, f32[8,128]{1,0:T(8,128)S(1)}, u32[]{:S(2)}, u32[]{:S(2)}) collective-permute-start(f32[8,128]{1,0:T(8,128)S(1)} %get-tuple-element.57.refs_0_), channel_id=1, source_target_pairs={{0,12},{1,13},{2,14},{3,15},{4,8},{5,9},{6,10},{7,11},{8,4},{9,5},... | collective-permute-start | bytes 12296 | tf_op jit(solution)/shard_map/ppermute | solution.py:23
  97.1 2.4 %collective-permute-start.37 = (f32[8,128]{1,0:T(8,128)S(1)}, f32[8,128]{1,0:T(8,128)S(1)}, u32[]{:S(2)}, u32[]{:S(2)}) collective-permute-start(f32[8,128]{1,0:T(8,128)S(1)} %get-tuple-element.57.refs_0_), channel_id=1, source_target_pairs={{0,4},{1,5},{2,6},{3,7},{4,0},{5,1},{6,2},{7,3},{8,12},{9,13},{10,... | collective-permute-start | bytes 12296 | tf_op jit(solution)/shard_map/ppermute | solution.py:23
  (92 shorter events, 36.4 us)
Async XLA Ops:
  2.3 12.6 %collective-permute-start.1 = (bf16[8,8,96,128]{3,2,1,0:T(8,128)(2,1)S(1)}, bf16[8,8,96,128]{3,2,1,0:T(8,128)(2,1)S(1)}, u32[]{:S(2)}, u32[]{:S(2)}) collective-permute-start(bf16[8,8,96,128]{3,2,1,0:T(8,128)(2,1)S(1)} %dynamic-slice_bitcast_fusion), channel_id=1, source_target_pairs={{0,1},{1,0},{2,3},{3,2},{4,5},{5,4},{6,7},{7,6},{8,9},{9,8},{10,11... | collective-permute-start | bytes 4718600 | tf_op jit(solution)/shard_map/ppermute | solution.py:23
  3.0 7.9 %collective-permute-start = (bf16[16,2304]{1,0:T(8,128)(2,1)S(1)}, bf16[16,2304]{1,0:T(8,128)(2,1)S(1)}, u32[]{:S(2)}, u32[]{:S(2)}) collective-permute-start(bf16[16,2304]{1,0:T(8,128)(2,1)S(1)} %get-tuple-element.33), channel_id=1, source_target_pairs={{0,12},{1,13},{2,14},{3,15},{4,8},{5,9},{6,10},{7,11},{8,4},{9,5},... | collective-permute-start | bytes 221192 | tf_op jit(solution)/shard_map/ppermute | solution.py:23
  7.6 7.1 %collective-permute-start.3 = (bf16[16,2304]{1,0:T(8,128)(2,1)S(1)}, bf16[16,2304]{1,0:T(8,128)(2,1)S(1)}, u32[]{:S(2)}, u32[]{:S(2)}) collective-permute-start(bf16[16,2304]{1,0:T(8,128)(2,1)S(1)} %get-tuple-element.34), channel_id=1, source_target_pairs={{0,6},{1,7},{2,4},{3,5},{4,2},{5,3},{6,0},{7,1},{8,14},{9,15},{10,... | collective-permute-start | bytes 221192 | tf_op jit(solution)/shard_map/ppermute | solution.py:23
  8.1 9.7 %collective-permute-start.5 = (bf16[16,2304]{1,0:T(8,128)(2,1)S(1)}, bf16[16,2304]{1,0:T(8,128)(2,1)S(1)}, u32[]{:S(2)}, u32[]{:S(2)}) collective-permute-start(bf16[16,2304]{1,0:T(8,128)(2,1)S(1)} %get-tuple-element.35), channel_id=1, source_target_pairs={{0,14},{1,15},{2,12},{3,13},{4,10},{5,11},{6,8},{7,9},{8,6},{9,7},... | collective-permute-start | bytes 221192 | tf_op jit(solution)/shard_map/ppermute | solution.py:23
  9.4 10.6 %collective-permute-start.13 = (bf16[16,2304]{1,0:T(8,128)(2,1)S(1)}, bf16[16,2304]{1,0:T(8,128)(2,1)S(1)}, u32[]{:S(2)}, u32[]{:S(2)}) collective-permute-start(bf16[16,2304]{1,0:T(8,128)(2,1)S(1)} %get-tuple-element.39), channel_id=1, source_target_pairs={{0,4},{1,5},{2,6},{3,7},{4,0},{5,1},{6,2},{7,3},{8,12},{9,13},{10,... | collective-permute-start | bytes 221192 | tf_op jit(solution)/shard_map/ppermute | solution.py:23
  10.8 11.3 %collective-permute-start.7 = (bf16[16,2304]{1,0:T(8,128)(2,1)S(1)}, bf16[16,2304]{1,0:T(8,128)(2,1)S(1)}, u32[]{:S(2)}, u32[]{:S(2)}) collective-permute-start(bf16[16,2304]{1,0:T(8,128)(2,1)S(1)} %get-tuple-element.36), channel_id=1, source_target_pairs={{0,10},{1,11},{2,8},{3,9},{4,14},{5,15},{6,12},{7,13},{8,2},{9,3},... | collective-permute-start | bytes 221192 | tf_op jit(solution)/shard_map/ppermute | solution.py:23
  14.8 10.9 %collective-permute-start.9 = (bf16[16,2304]{1,0:T(8,128)(2,1)S(1)}, bf16[16,2304]{1,0:T(8,128)(2,1)S(1)}, u32[]{:S(2)}, u32[]{:S(2)}) collective-permute-start(bf16[16,2304]{1,0:T(8,128)(2,1)S(1)} %get-tuple-element.37), channel_id=1, source_target_pairs={{0,8},{1,9},{2,10},{3,11},{4,12},{5,13},{6,14},{7,15},{8,0},{9,1},... | collective-permute-start | bytes 221192 | tf_op jit(solution)/shard_map/ppermute | solution.py:23
  14.9 12.4 %collective-permute-start.11 = (bf16[16,2304]{1,0:T(8,128)(2,1)S(1)}, bf16[16,2304]{1,0:T(8,128)(2,1)S(1)}, u32[]{:S(2)}, u32[]{:S(2)}) collective-permute-start(bf16[16,2304]{1,0:T(8,128)(2,1)S(1)} %get-tuple-element.38), channel_id=1, source_target_pairs={{0,2},{1,3},{2,0},{3,1},{4,6},{5,7},{6,4},{7,5},{8,10},{9,11},{10,... | collective-permute-start | bytes 221192 | tf_op jit(solution)/shard_map/ppermute | solution.py:23
  17.9 12.4 %collective-permute-start.2 = (f32[96,128]{1,0:T(8,128)S(1)}, f32[96,128]{1,0:T(8,128)S(1)}, u32[]{:S(2)}, u32[]{:S(2)}) collective-permute-start(f32[96,128]{1,0:T(8,128)S(1)} %shard_map.60), channel_id=1, source_target_pairs={{0,12},{1,13},{2,14},{3,15},{4,8},{5,9},{6,10},{7,11},{8,4},{9,5},... | collective-permute-start | bytes 147464 | tf_op jit(solution)/shard_map/ppermute | solution.py:23
  20.0 11.2 %collective-permute-start.4 = (f32[96,128]{1,0:T(8,128)S(1)}, f32[96,128]{1,0:T(8,128)S(1)}, u32[]{:S(2)}, u32[]{:S(2)}) collective-permute-start(f32[96,128]{1,0:T(8,128)S(1)} %shard_map.61), channel_id=1, source_target_pairs={{0,6},{1,7},{2,4},{3,5},{4,2},{5,3},{6,0},{7,1},{8,14},{9,15},{10,... | collective-permute-start | bytes 147464 | tf_op jit(solution)/shard_map/ppermute | solution.py:23
  22.1 9.6 %collective-permute-start.6 = (f32[96,128]{1,0:T(8,128)S(1)}, f32[96,128]{1,0:T(8,128)S(1)}, u32[]{:S(2)}, u32[]{:S(2)}) collective-permute-start(f32[96,128]{1,0:T(8,128)S(1)} %shard_map.62), channel_id=1, source_target_pairs={{0,14},{1,15},{2,12},{3,13},{4,10},{5,11},{6,8},{7,9},{8,6},{9,7},... | collective-permute-start | bytes 147464 | tf_op jit(solution)/shard_map/ppermute | solution.py:23
  25.7 6.1 %collective-permute-start.8 = (f32[96,128]{1,0:T(8,128)S(1)}, f32[96,128]{1,0:T(8,128)S(1)}, u32[]{:S(2)}, u32[]{:S(2)}) collective-permute-start(f32[96,128]{1,0:T(8,128)S(1)} %shard_map.63), channel_id=1, source_target_pairs={{0,10},{1,11},{2,8},{3,9},{4,14},{5,15},{6,12},{7,13},{8,2},{9,3},... | collective-permute-start | bytes 147464 | tf_op jit(solution)/shard_map/ppermute | solution.py:23
  35.4 13.1 %collective-permute-start.16 = (bf16[8,96,128]{2,1,0:T(8,128)(2,1)S(1)}, bf16[8,96,128]{2,1,0:T(8,128)(2,1)S(1)}, u32[]{:S(2)}, u32[]{:S(2)}) collective-permute-start(bf16[8,96,128]{2,1,0:T(8,128)(2,1)S(1)} %get-tuple-element.41.own_ref), channel_id=1, source_target_pairs={{0,7},{1,2},{2,1},{3,4},{4,3},{5,6},{6,5},{7,0},{8,15},{9,10},{10,... | collective-permute-start | bytes 589832 | tf_op jit(solution)/shard_map/ppermute | solution.py:23
  35.4 13.0 %collective-permute-start.15 = (bf16[8,96,128]{2,1,0:T(8,128)(2,1)S(1)}, bf16[8,96,128]{2,1,0:T(8,128)(2,1)S(1)}, u32[]{:S(2)}, u32[]{:S(2)}) collective-permute-start(bf16[8,96,128]{2,1,0:T(8,128)(2,1)S(1)} %get-tuple-element.41.own_ref), channel_id=1, source_target_pairs={{0,1},{1,0},{2,3},{3,2},{4,5},{5,4},{6,7},{7,6},{8,9},{9,8},{10,11... | collective-permute-start | bytes 589832 | tf_op jit(solution)/shard_map/ppermute | solution.py:23
  36.7 10.1 %collective-permute-start.17 = (bf16[4,96,128]{2,1,0:T(8,128)(2,1)S(1)}, bf16[4,96,128]{2,1,0:T(8,128)(2,1)S(1)}, u32[]{:S(2)}, u32[]{:S(2)}) collective-permute-start(bf16[4,96,128]{2,1,0:T(8,128)(2,1)S(1)} %shard_map.70), channel_id=1, source_target_pairs={{8,0},{9,1},{10,2},{11,3},{12,4},{13,5},{14,6},{15,7},{0,8},{1,9},... | collective-permute-start | bytes 294920 | tf_op jit(solution)/shard_map/ppermute | solution.py:23
  37.4 11.1 %collective-permute-start.18 = (bf16[4,96,128]{2,1,0:T(8,128)(2,1)S(1)}, bf16[4,96,128]{2,1,0:T(8,128)(2,1)S(1)}, u32[]{:S(2)}, u32[]{:S(2)}) collective-permute-start(bf16[4,96,128]{2,1,0:T(8,128)(2,1)S(1)} %get-tuple-element.43), channel_id=1, source_target_pairs={{8,0},{9,1},{10,2},{11,3},{12,4},{13,5},{14,6},{15,7},{0,8},{1,9},... | collective-permute-start | bytes 294920 | tf_op jit(solution)/shard_map/ppermute | solution.py:23
  49.1 5.5 %collective-permute-start.21 = (f32[8,128]{1,0:T(8,128)S(1)}, f32[8,128]{1,0:T(8,128)S(1)}, u32[]{:S(2)}, u32[]{:S(2)}) collective-permute-start(f32[8,128]{1,0:T(8,128)S(1)} %get-tuple-element.44.refs_0_), channel_id=1, source_target_pairs={{0,12},{1,13},{2,14},{3,15},{4,8},{5,9},{6,10},{7,11},{8,4},{9,5},... | collective-permute-start | bytes 12296 | tf_op jit(solution)/shard_map/ppermute | solution.py:23
  59.2 12.1 %collective-permute-start.27 = (bf16[8,96,128]{2,1,0:T(8,128)(2,1)S(1)}, bf16[8,96,128]{2,1,0:T(8,128)(2,1)S(1)}, u32[]{:S(2)}, u32[]{:S(2)}) collective-permute-start(bf16[8,96,128]{2,1,0:T(8,128)(2,1)S(1)} %get-tuple-element.46.own_ref), channel_id=1, source_target_pairs={{8,0},{9,1},{10,2},{11,3},{12,4},{13,5},{14,6},{15,7},{0,8},{1,9},... | collective-permute-start | bytes 589832 | tf_op jit(solution)/shard_map/ppermute | solution.py:23
  61.2 10.1 %collective-permute-start.26 = (bf16[8,96,128]{2,1,0:T(8,128)(2,1)S(1)}, bf16[8,96,128]{2,1,0:T(8,128)(2,1)S(1)}, u32[]{:S(2)}, u32[]{:S(2)}) collective-permute-start(bf16[8,96,128]{2,1,0:T(8,128)(2,1)S(1)} %get-tuple-element.46.own_ref), channel_id=1, source_target_pairs={{0,7},{1,2},{2,1},{3,4},{4,3},{5,6},{6,5},{7,0},{8,15},{9,10},{10,... | collective-permute-start | bytes 589832 | tf_op jit(solution)/shard_map/ppermute | solution.py:23
  61.7 9.5 %collective-permute-start.25 = (bf16[8,96,128]{2,1,0:T(8,128)(2,1)S(1)}, bf16[8,96,128]{2,1,0:T(8,128)(2,1)S(1)}, u32[]{:S(2)}, u32[]{:S(2)}) collective-permute-start(bf16[8,96,128]{2,1,0:T(8,128)(2,1)S(1)} %get-tuple-element.46.own_ref), channel_id=1, source_target_pairs={{0,1},{1,0},{2,3},{3,2},{4,5},{5,4},{6,7},{7,6},{8,9},{9,8},{10,11... | collective-permute-start | bytes 589832 | tf_op jit(solution)/shard_map/ppermute | solution.py:23
  82.3 12.1 %collective-permute-start.36 = (bf16[8,96,128]{2,1,0:T(8,128)(2,1)S(1)}, bf16[8,96,128]{2,1,0:T(8,128)(2,1)S(1)}, u32[]{:S(2)}, u32[]{:S(2)}) collective-permute-start(bf16[8,96,128]{2,1,0:T(8,128)(2,1)S(1)} %get-tuple-element.54.own_ref), channel_id=1, source_target_pairs={{8,0},{9,1},{10,2},{11,3},{12,4},{13,5},{14,6},{15,7},{0,8},{1,9},... | collective-permute-start | bytes 589832 | tf_op jit(solution)/shard_map/ppermute | solution.py:23
  84.3 10.1 %collective-permute-start.35 = (bf16[8,96,128]{2,1,0:T(8,128)(2,1)S(1)}, bf16[8,96,128]{2,1,0:T(8,128)(2,1)S(1)}, u32[]{:S(2)}, u32[]{:S(2)}) collective-permute-start(bf16[8,96,128]{2,1,0:T(8,128)(2,1)S(1)} %get-tuple-element.54.own_ref), channel_id=1, source_target_pairs={{0,7},{1,2},{2,1},{3,4},{4,3},{5,6},{6,5},{7,0},{8,15},{9,10},{10,... | collective-permute-start | bytes 589832 | tf_op jit(solution)/shard_map/ppermute | solution.py:23
  84.9 9.6 %collective-permute-start.34 = (bf16[8,96,128]{2,1,0:T(8,128)(2,1)S(1)}, bf16[8,96,128]{2,1,0:T(8,128)(2,1)S(1)}, u32[]{:S(2)}, u32[]{:S(2)}) collective-permute-start(bf16[8,96,128]{2,1,0:T(8,128)(2,1)S(1)} %get-tuple-element.54.own_ref), channel_id=1, source_target_pairs={{0,1},{1,0},{2,3},{3,2},{4,5},{5,4},{6,7},{7,6},{8,9},{9,8},{10,11... | collective-permute-start | bytes 589832 | tf_op jit(solution)/shard_map/ppermute | solution.py:23
  95.1 5.5 %collective-permute-start.39 = (f32[8,128]{1,0:T(8,128)S(1)}, f32[8,128]{1,0:T(8,128)S(1)}, u32[]{:S(2)}, u32[]{:S(2)}) collective-permute-start(f32[8,128]{1,0:T(8,128)S(1)} %get-tuple-element.57.refs_0_), channel_id=1, source_target_pairs={{0,12},{1,13},{2,14},{3,15},{4,8},{5,9},{6,10},{7,11},{8,4},{9,5},... | collective-permute-start | bytes 12296 | tf_op jit(solution)/shard_map/ppermute | solution.py:23
  (22 other events, 101.3 us)
